TPU v7x, 128 devices: a whole 4x4x4 slice. The times are simulated.
128 devices in a mesh: chip: 32 (over x, z, core), cores: 4 (over y).
Axes of the slice: x: 4, y: 4, z: 4, core: 2. Of those that a mesh axis runs over, the one named last changes fastest.
Arguments:
- start_offset: float32 [4096, 512], P(('chip', 'cores')), may hold values from -4 to 4
- chars: float32 [4096, 6, 512], P(('chip', 'cores')), may hold values from -3 to 3
- share_rel: float32 [4096, 512], P(('chip', 'cores')), may hold values from -2.5 to 2.5
- draws: float32 [4096, 6, 768], P(('chip', 'cores')), may hold values from -3 to 3
- sigma: float32 [6], replicated, may hold values from 0.1 to 0.8
- counts: int32 [4096], P(('chip', 'cores')), may hold values from 8 to 512, as said below
- converged: int32 [4096], P(('chip', 'cores')), may hold values from 0 to 1, as said below
- destination: int32 [4096], P(('chip', 'cores')), may hold values from -1 to 1535, as said below
Outputs:
- delta: float32 [4096, 512], P(('chip', 'cores'))
- work_delta: float32 [1536, 512], P(('chip', 'cores'))
- step_norm: float32 [], replicated
Inputs may be any that keep to these rules, and one draw needn't show every extreme that they name: `counts`: on every device one market has exactly 512 products. On every device between 4 and 20 markets have converged 0. destination is -1 exactly where converged is 1; otherwise it is v * 12 + s with s < 12 and v a device (numbered chip-major over chip and cores) with the same cores index as the market's own device. Every device's 12 slots are each named exactly once. At most 1 markets of one device name slots of one other device, and some pair reaches that number.
All inputs are finite; a program needn't handle non-finite values.
Results may differ from a plain program's by a relative error of at most 0.0003.
Values sent between devices are 32-bit elements; how exact they have to be, the bound alone decides.
No kernel may reach another device: no remote copies, remote signals or barrier semaphores. Data moves between devices by JAX's collectives and lax.ppermute only.
A program may use at most 64 MiB of HBM per device.

v0:
```python
import functools

import jax
import jax.numpy as jnp
from jax import lax
from jax.sharding import Mesh
from jax.sharding import PartitionSpec as P

TAIL_ITERS = 4
CHIP = ("chip_0", "chip_1", "chip_2")
CHIP_CORES = ("chip_0", "chip_1", "chip_2", "cores")


def by_axis(x, axes):
    return functools.reduce(lax.psum, axes, x)


def shock_table(features, market_draws, live_rows, coef_scale):
    spread = jnp.einsum(
        "kj,kr->jr", features * coef_scale[:, None], market_draws, precision=lax.Precision.HIGHEST
    )
    return jnp.exp(spread) * live_rows[:, None]


def contract(deltas, table, log_share, live_rows):
    utility = jnp.exp(deltas)[:, None] * table
    inside = jnp.sum(utility, axis=0)
    predicted = jnp.mean(utility / (1.0 + inside)[None, :], axis=1)
    updated = deltas + log_share - jnp.log(jnp.where(live_rows > 0, predicted, 1.0))
    return updated * live_rows


def grouped_map(handler, arrays):
    total = arrays[0].shape[0]
    group = 1
    for option in (8, 4, 2):
        if total % option == 0:
            group = option
            break
    shaped = tuple((a.reshape((total // group, group) + a.shape[1:]) for a in arrays))
    result = lax.map(jax.vmap(handler), shaped)
    return result.reshape((total,) + result.shape[2:])


def local(start_offset, chars, share_rel, draws, sigma, counts, converged, destination):
    row_count = start_offset.shape[1]
    market_count = counts.shape[0]
    chip_count = lax.axis_size(CHIP)
    processor_total = lax.axis_size("cores")
    slot_count = 3 * market_count // 8
    busy_room = 5 * market_count // 8
    pair_room = (busy_room + chip_count - 1) // chip_count
    buffer_rows = chip_count * pair_room
    positions = jnp.arange(row_count, dtype=jnp.int32)
    live_mask = (positions[None, :] < counts[:, None]).astype(jnp.float32)
    log_obs = share_rel - jnp.log(counts.astype(jnp.float32))[:, None] - 1.5
    initial = (log_obs + start_offset) * live_mask

    def remaining_steps(packed):
        deltas, features, log_share, market_draws, live_rows = packed
        table = shock_table(features, market_draws, live_rows, sigma)
        latest = deltas
        for step in range(TAIL_ITERS):
            latest = contract(latest, table, log_share, live_rows)
        return latest

    def two_steps(packed):
        deltas, features, log_share, market_draws, live_rows = packed
        table = shock_table(features, market_draws, live_rows, sigma)
        initial_update = contract(deltas, table, log_share, live_rows)
        return contract(initial_update, table, log_share, live_rows)

    keep_mask = converged == 1
    moving = jnp.logical_not(keep_mask)
    target_chip = destination // slot_count // processor_total
    market_line = jnp.arange(market_count, dtype=jnp.int32)
    earlier = (
        (target_chip[:, None] == target_chip[None, :])
        & moving[None, :]
        & (market_line[None, :] < market_line[:, None])
    )
    pair_rank = jnp.sum(earlier.astype(jnp.int32), axis=1)
    send_place = jnp.where(moving, target_chip * pair_room + pair_rank, buffer_rows)
    slot_values = jnp.where(moving, destination % slot_count, slot_count)
    slot_ids = (
        jnp.full((buffer_rows,), slot_count, jnp.int32)
        .at[send_place]
        .set(slot_values, mode="drop")
        .reshape(chip_count, pair_room)
    )
    local_active = jnp.sum(jnp.where(moving, counts, 0))
    second = grouped_map(two_steps, (initial, chars, log_obs, draws, live_mask))
    busy_rank = jnp.cumsum(moving.astype(jnp.int32)) - 1
    busy_place = jnp.where(moving, busy_rank, busy_room)

    def compact(values):
        return (
            jnp.zeros((busy_room,) + values.shape[1:], values.dtype)
            .at[busy_place]
            .set(values, mode="drop")
        )

    busy_final = grouped_map(
        remaining_steps,
        (compact(second), compact(chars), compact(log_obs), compact(draws), compact(live_mask)),
    )
    final_home = busy_final[jnp.minimum(busy_place, busy_room - 1)]
    change = jnp.sum(jnp.where(moving[:, None], (final_home - second) ** 2, 0.0))
    placed = (
        jnp.zeros((buffer_rows,) + final_home.shape[1:], final_home.dtype)
        .at[send_place]
        .set(final_home, mode="drop")
    )
    values = lax.all_to_all(
        placed.reshape((chip_count, pair_room) + final_home.shape[1:]),
        CHIP,
        split_axis=0,
        concat_axis=0,
        tiled=True,
    )
    flattened = values.reshape((buffer_rows,) + values.shape[2:])
    work_delta = (
        jnp.zeros((slot_count,) + flattened.shape[1:], flattened.dtype)
        .at[
            lax.all_to_all(slot_ids, CHIP, split_axis=0, concat_axis=0, tiled=True).reshape(
                buffer_rows
            )
        ]
        .set(flattened, mode="drop")
    )
    deltas = jnp.where(keep_mask[:, None], second, final_home)
    total_change, total_active = (by_axis(change, CHIP_CORES), by_axis(local_active, CHIP_CORES))
    step_norm = jnp.sqrt(total_change / jnp.asarray(total_active).astype(jnp.float32))
    return (deltas, work_delta, step_norm)


def solution(mesh):
    finer = Mesh(
        mesh.devices.reshape(4, 4, 2, mesh.shape["cores"]), ("chip_0", "chip_1", "chip_2", "cores")
    )
    return jax.shard_map(
        local,
        mesh=finer,
        in_specs=(
            P(CHIP_CORES, None),
            P(CHIP_CORES, None, None),
            P(CHIP_CORES, None),
            P(CHIP_CORES, None, None),
            P(),
            P(CHIP_CORES),
            P(CHIP_CORES),
            P(CHIP_CORES),
        ),
        out_specs=(P(CHIP_CORES, None), P(CHIP_CORES, None), P()),
        check_vma=False,
    )
```

profile of v0, /device:TPU:1, one launch (start us, length us, event | category | flops | bytes accessed | tf_op | source)
XLA Modules:
  0.0 264.4 jit_solution(9670184420593854006)
XLA Ops:
  3.9 1.4 copy.39
  5.3 1.2 copy.38
  7.6 92.1 %while.22 = (s32[]{:T(128)}, f32[4,8,512]{2,1,0:T(8,128)S(1)}, f32[4,8,512]{2,1,0:T(8,128)S(1)}, f32[4,8,512]{2,1,0:T(8,128)S(1)}, f32[4,8,512]{2,1,0:T(8,128)S(...) while((s32[]{:T(128)}, f32[4,8,512]{2,1,0:T(8,128)S(1)}, ...), condition=%wide.region_5.6_spmd.clone, body=%wide.region_0.5_spmd.sunk.clone | while | flops 270618624 | bytes 51267168 | solution.py:41
  7.7 12.7 %multiply_reduce_fusion.18 = (f32[8,768]{1,0:T(8,128)S(1)}, f32[8,512,768]{2,1,0:T(8,128)S(1)}) fusion(f32[8,512]{1,0:T(8,128)S(1)} %get-tuple-element.262, f32[8,512]{1,0:T(8,128)S(1)} %get-tuple-element.263, f32[4,8,6,768]{3,2,1,0:T(8,128)S(1)} %get-tuple-element.320, s32[]{:T(128)} %get-tuple-element.305, ...), kind=kOutput, calls=%fused_computation.13.clone.1.clone | convolution fusion | flops 235948032 | bytes 12969472 | tf_op jit(solution)/shard_map/while/body/eval_jaxpr/vmap(kj,kr->jr)/dot_general | solution.py:19
  20.4 3.6 %divide_reduce_fusion.18 = f32[8,512]{1,0:T(8,128)S(1)} fusion(f32[8,512,768]{2,1,0:T(8,128)S(1)} %get-tuple-element.264, f32[8,768]{1,0:T(8,128)S(1)} %broadcast_add_fusion.18, f32[8,512]{1,0:T(8,128)S(1)} %get-tuple-element.262, f32[8,512]{1,0:T(8,128)S(1)} %get-tuple-element.263), kind=kLoop, calls=%fused_computation.11.clone.1.clone | loop fusion | flops 12578816 | bytes 12656640 | tf_op jit(solution)/shard_map/while/body/eval_jaxpr/vmap()/reduce_sum | solution.py:28
  24.1 2.8 %multiply_reduce_fusion.19 = f32[8,768]{1,0:T(8,128)S(1)} fusion(f32[8,512,768]{2,1,0:T(8,128)S(1)} %get-tuple-element.264, f32[8,512]{1,0:T(8,128)S(1)} %fusion.87, f32[8,512]{1,0:T(8,128)S(1)} %get-tuple-element.262), kind=kLoop, calls=%fused_computation.12.clone.1.clone | loop fusion | flops 9431040 | bytes 12640256 | tf_op jit(solution)/shard_map/while/body/eval_jaxpr/vmap()/reduce_sum | solution.py:27
  26.9 3.6 %divide_reduce_fusion.19 = f32[8,512]{1,0:T(8,128)S(1)} fusion(f32[8,512,768]{2,1,0:T(8,128)S(1)} %get-tuple-element.264, f32[8,768]{1,0:T(8,128)S(1)} %broadcast_add_fusion.19, f32[8,512]{1,0:T(8,128)S(1)} %fusion.87, f32[8,512]{1,0:T(8,128)S(1)} %get-tuple-element.262), kind=kLoop, calls=%fused_computation.10.clone.1.clone | loop fusion | flops 12578816 | bytes 12656640 | tf_op jit(solution)/shard_map/while/body/eval_jaxpr/vmap()/reduce_sum | solution.py:28
  30.7 12.7 %multiply_reduce_fusion.18 = (f32[8,768]{1,0:T(8,128)S(1)}, f32[8,512,768]{2,1,0:T(8,128)S(1)}) fusion(f32[8,512]{1,0:T(8,128)S(1)} %get-tuple-element.262, f32[8,512]{1,0:T(8,128)S(1)} %get-tuple-element.263, f32[4,8,6,768]{3,2,1,0:T(8,128)S(1)} %get-tuple-element.320, s32[]{:T(128)} %get-tuple-element.305, ...), kind=kOutput, calls=%fused_computation.13.clone.1.clone | convolution fusion | flops 235948032 | bytes 12969472 | tf_op jit(solution)/shard_map/while/body/eval_jaxpr/vmap(kj,kr->jr)/dot_general | solution.py:19
  43.4 3.6 %divide_reduce_fusion.18 = f32[8,512]{1,0:T(8,128)S(1)} fusion(f32[8,512,768]{2,1,0:T(8,128)S(1)} %get-tuple-element.264, f32[8,768]{1,0:T(8,128)S(1)} %broadcast_add_fusion.18, f32[8,512]{1,0:T(8,128)S(1)} %get-tuple-element.262, f32[8,512]{1,0:T(8,128)S(1)} %get-tuple-element.263), kind=kLoop, calls=%fused_computation.11.clone.1.clone | loop fusion | flops 12578816 | bytes 12656640 | tf_op jit(solution)/shard_map/while/body/eval_jaxpr/vmap()/reduce_sum | solution.py:28
  47.1 2.8 %multiply_reduce_fusion.19 = f32[8,768]{1,0:T(8,128)S(1)} fusion(f32[8,512,768]{2,1,0:T(8,128)S(1)} %get-tuple-element.264, f32[8,512]{1,0:T(8,128)S(1)} %fusion.87, f32[8,512]{1,0:T(8,128)S(1)} %get-tuple-element.262), kind=kLoop, calls=%fused_computation.12.clone.1.clone | loop fusion | flops 9431040 | bytes 12640256 | tf_op jit(solution)/shard_map/while/body/eval_jaxpr/vmap()/reduce_sum | solution.py:27
  49.9 3.6 %divide_reduce_fusion.19 = f32[8,512]{1,0:T(8,128)S(1)} fusion(f32[8,512,768]{2,1,0:T(8,128)S(1)} %get-tuple-element.264, f32[8,768]{1,0:T(8,128)S(1)} %broadcast_add_fusion.19, f32[8,512]{1,0:T(8,128)S(1)} %fusion.87, f32[8,512]{1,0:T(8,128)S(1)} %get-tuple-element.262), kind=kLoop, calls=%fused_computation.10.clone.1.clone | loop fusion | flops 12578816 | bytes 12656640 | tf_op jit(solution)/shard_map/while/body/eval_jaxpr/vmap()/reduce_sum | solution.py:28
  53.6 12.7 %multiply_reduce_fusion.18 = (f32[8,768]{1,0:T(8,128)S(1)}, f32[8,512,768]{2,1,0:T(8,128)S(1)}) fusion(f32[8,512]{1,0:T(8,128)S(1)} %get-tuple-element.262, f32[8,512]{1,0:T(8,128)S(1)} %get-tuple-element.263, f32[4,8,6,768]{3,2,1,0:T(8,128)S(1)} %get-tuple-element.320, s32[]{:T(128)} %get-tuple-element.305, ...), kind=kOutput, calls=%fused_computation.13.clone.1.clone | convolution fusion | flops 235948032 | bytes 12969472 | tf_op jit(solution)/shard_map/while/body/eval_jaxpr/vmap(kj,kr->jr)/dot_general | solution.py:19
  66.4 3.6 %divide_reduce_fusion.18 = f32[8,512]{1,0:T(8,128)S(1)} fusion(f32[8,512,768]{2,1,0:T(8,128)S(1)} %get-tuple-element.264, f32[8,768]{1,0:T(8,128)S(1)} %broadcast_add_fusion.18, f32[8,512]{1,0:T(8,128)S(1)} %get-tuple-element.262, f32[8,512]{1,0:T(8,128)S(1)} %get-tuple-element.263), kind=kLoop, calls=%fused_computation.11.clone.1.clone | loop fusion | flops 12578816 | bytes 12656640 | tf_op jit(solution)/shard_map/while/body/eval_jaxpr/vmap()/reduce_sum | solution.py:28
  70.1 2.8 %multiply_reduce_fusion.19 = f32[8,768]{1,0:T(8,128)S(1)} fusion(f32[8,512,768]{2,1,0:T(8,128)S(1)} %get-tuple-element.264, f32[8,512]{1,0:T(8,128)S(1)} %fusion.87, f32[8,512]{1,0:T(8,128)S(1)} %get-tuple-element.262), kind=kLoop, calls=%fused_computation.12.clone.1.clone | loop fusion | flops 9431040 | bytes 12640256 | tf_op jit(solution)/shard_map/while/body/eval_jaxpr/vmap()/reduce_sum | solution.py:27
  72.9 3.6 %divide_reduce_fusion.19 = f32[8,512]{1,0:T(8,128)S(1)} fusion(f32[8,512,768]{2,1,0:T(8,128)S(1)} %get-tuple-element.264, f32[8,768]{1,0:T(8,128)S(1)} %broadcast_add_fusion.19, f32[8,512]{1,0:T(8,128)S(1)} %fusion.87, f32[8,512]{1,0:T(8,128)S(1)} %get-tuple-element.262), kind=kLoop, calls=%fused_computation.10.clone.1.clone | loop fusion | flops 12578816 | bytes 12656640 | tf_op jit(solution)/shard_map/while/body/eval_jaxpr/vmap()/reduce_sum | solution.py:28
  76.6 12.7 %multiply_reduce_fusion.18 = (f32[8,768]{1,0:T(8,128)S(1)}, f32[8,512,768]{2,1,0:T(8,128)S(1)}) fusion(f32[8,512]{1,0:T(8,128)S(1)} %get-tuple-element.262, f32[8,512]{1,0:T(8,128)S(1)} %get-tuple-element.263, f32[4,8,6,768]{3,2,1,0:T(8,128)S(1)} %get-tuple-element.320, s32[]{:T(128)} %get-tuple-element.305, ...), kind=kOutput, calls=%fused_computation.13.clone.1.clone | convolution fusion | flops 235948032 | bytes 12969472 | tf_op jit(solution)/shard_map/while/body/eval_jaxpr/vmap(kj,kr->jr)/dot_general | solution.py:19
  89.4 3.6 %divide_reduce_fusion.18 = f32[8,512]{1,0:T(8,128)S(1)} fusion(f32[8,512,768]{2,1,0:T(8,128)S(1)} %get-tuple-element.264, f32[8,768]{1,0:T(8,128)S(1)} %broadcast_add_fusion.18, f32[8,512]{1,0:T(8,128)S(1)} %get-tuple-element.262, f32[8,512]{1,0:T(8,128)S(1)} %get-tuple-element.263), kind=kLoop, calls=%fused_computation.11.clone.1.clone | loop fusion | flops 12578816 | bytes 12656640 | tf_op jit(solution)/shard_map/while/body/eval_jaxpr/vmap()/reduce_sum | solution.py:28
  93.0 2.8 %multiply_reduce_fusion.19 = f32[8,768]{1,0:T(8,128)S(1)} fusion(f32[8,512,768]{2,1,0:T(8,128)S(1)} %get-tuple-element.264, f32[8,512]{1,0:T(8,128)S(1)} %fusion.87, f32[8,512]{1,0:T(8,128)S(1)} %get-tuple-element.262), kind=kLoop, calls=%fused_computation.12.clone.1.clone | loop fusion | flops 9431040 | bytes 12640256 | tf_op jit(solution)/shard_map/while/body/eval_jaxpr/vmap()/reduce_sum | solution.py:27
  95.9 3.6 %divide_reduce_fusion.19 = f32[8,512]{1,0:T(8,128)S(1)} fusion(f32[8,512,768]{2,1,0:T(8,128)S(1)} %get-tuple-element.264, f32[8,768]{1,0:T(8,128)S(1)} %broadcast_add_fusion.19, f32[8,512]{1,0:T(8,128)S(1)} %fusion.87, f32[8,512]{1,0:T(8,128)S(1)} %get-tuple-element.262), kind=kLoop, calls=%fused_computation.10.clone.1.clone | loop fusion | flops 12578816 | bytes 12656640 | tf_op jit(solution)/shard_map/while/body/eval_jaxpr/vmap()/reduce_sum | solution.py:28
  102.0 1.7 scatter_fusion.1
  103.7 1.6 scatter_fusion
  106.1 64.9 %while.23 = (s32[]{:T(128)}, f32[5,4,512]{2,1,0:T(4,128)S(1)}, f32[5,4,512]{2,1,0:T(4,128)S(1)}, f32[5,4,512]{2,1,0:T(4,128)S(1)}, f32[5,4,512]{2,1,0:T(4,128)S(...) while((s32[]{:T(128)}, f32[5,4,512]{2,1,0:T(4,128)S(1)}, ...), condition=%wide.region_21.22_spmd.clone, body=%wide.region_12.21_spmd.sunk.clone | while | flops 146370560 | bytes 51037804 | solution.py:41
  106.1 6.9 %multiply_reduce_fusion.20 = (f32[4,768]{1,0:T(4,128)S(1)}, f32[4,512,768]{2,1,0:T(8,128)S(1)}) fusion(f32[4,512]{1,0:T(4,128)S(1)} %bitcast_exponential_fusion.3, f32[4,512]{1,0:T(4,128)S(1)} %dynamic-slice_bitcast_fusion.4, f32[5,4,6,768]{3,2,1,0:T(8,128)S(1)} %get-tuple-element.344, s32[]{:T(128)} %get-tuple-element.329, ...), kind=kOutput, calls=%fused_computation.47.clone.1.clone | convolution fusion | flops 117974016 | bytes 6485504 | tf_op jit(solution)/shard_map/while/body/eval_jaxpr/vmap(kj,kr->jr)/dot_general | solution.py:19
  114.7 1.0 divide_reduce_fusion.21
  116.3 1.0 divide_reduce_fusion.22
  118.0 1.0 divide_reduce_fusion.23
  119.1 6.9 %multiply_reduce_fusion.20 = (f32[4,768]{1,0:T(4,128)S(1)}, f32[4,512,768]{2,1,0:T(8,128)S(1)}) fusion(f32[4,512]{1,0:T(4,128)S(1)} %bitcast_exponential_fusion.3, f32[4,512]{1,0:T(4,128)S(1)} %dynamic-slice_bitcast_fusion.4, f32[5,4,6,768]{3,2,1,0:T(8,128)S(1)} %get-tuple-element.344, s32[]{:T(128)} %get-tuple-element.329, ...), kind=kOutput, calls=%fused_computation.47.clone.1.clone | convolution fusion | flops 117974016 | bytes 6485504 | tf_op jit(solution)/shard_map/while/body/eval_jaxpr/vmap(kj,kr->jr)/dot_general | solution.py:19
  127.7 1.0 divide_reduce_fusion.21
  129.3 1.0 divide_reduce_fusion.22
  131.0 1.0 divide_reduce_fusion.23
  132.1 6.9 %multiply_reduce_fusion.20 = (f32[4,768]{1,0:T(4,128)S(1)}, f32[4,512,768]{2,1,0:T(8,128)S(1)}) fusion(f32[4,512]{1,0:T(4,128)S(1)} %bitcast_exponential_fusion.3, f32[4,512]{1,0:T(4,128)S(1)} %dynamic-slice_bitcast_fusion.4, f32[5,4,6,768]{3,2,1,0:T(8,128)S(1)} %get-tuple-element.344, s32[]{:T(128)} %get-tuple-element.329, ...), kind=kOutput, calls=%fused_computation.47.clone.1.clone | convolution fusion | flops 117974016 | bytes 6485504 | tf_op jit(solution)/shard_map/while/body/eval_jaxpr/vmap(kj,kr->jr)/dot_general | solution.py:19
  140.7 1.0 divide_reduce_fusion.21
  145.1 6.9 %multiply_reduce_fusion.20 = (f32[4,768]{1,0:T(4,128)S(1)}, f32[4,512,768]{2,1,0:T(8,128)S(1)}) fusion(f32[4,512]{1,0:T(4,128)S(1)} %bitcast_exponential_fusion.3, f32[4,512]{1,0:T(4,128)S(1)} %dynamic-slice_bitcast_fusion.4, f32[5,4,6,768]{3,2,1,0:T(8,128)S(1)} %get-tuple-element.344, s32[]{:T(128)} %get-tuple-element.329, ...), kind=kOutput, calls=%fused_computation.47.clone.1.clone | convolution fusion | flops 117974016 | bytes 6485504 | tf_op jit(solution)/shard_map/while/body/eval_jaxpr/vmap(kj,kr->jr)/dot_general | solution.py:19
  156.9 1.0 divide_reduce_fusion.23
  158.1 6.9 %multiply_reduce_fusion.20 = (f32[4,768]{1,0:T(4,128)S(1)}, f32[4,512,768]{2,1,0:T(8,128)S(1)}) fusion(f32[4,512]{1,0:T(4,128)S(1)} %bitcast_exponential_fusion.3, f32[4,512]{1,0:T(4,128)S(1)} %dynamic-slice_bitcast_fusion.4, f32[5,4,6,768]{3,2,1,0:T(8,128)S(1)} %get-tuple-element.344, s32[]{:T(128)} %get-tuple-element.329, ...), kind=kOutput, calls=%fused_computation.47.clone.1.clone | convolution fusion | flops 117974016 | bytes 6485504 | tf_op jit(solution)/shard_map/while/body/eval_jaxpr/vmap(kj,kr->jr)/dot_general | solution.py:19
  169.9 1.0 divide_reduce_fusion.23
  172.3 9.8 %psum.56 = f32[]{:T(128)} all-reduce(f32[]{:T(128)} %fusion.50), channel_id=1, replica_groups=mesh['chip_0'=4,'chip_1'=4,'chip_2'=2,'cores'=4] {'chip_0'}, use_global_device_ids=true, to_apply=%region_27.28 | all-reduce | flops 1 | bytes 8 | tf_op jit(solution)/shard_map/psum | solution.py:15
  182.2 10.3 %psum.57 = f32[]{:T(128)} all-reduce(f32[]{:T(128)} %psum.56), channel_id=1, replica_groups=mesh['chip_0'=4,'chip_1'=4,'chip_2'=2,'cores'=4] {'chip_1'}, use_global_device_ids=true, to_apply=%region_28.29 | all-reduce | flops 1 | bytes 8 | tf_op jit(solution)/shard_map/psum | solution.py:15
  192.5 5.6 %psum.60 = s32[]{:T(128)} all-reduce(s32[]{:T(128)} %get-tuple-element.133), channel_id=1, replica_groups=mesh['chip_0'=4,'chip_1'=4,'chip_2'=2,'cores'=4] {'chip_0'}, use_global_device_ids=true, to_apply=%region_32.33 | all-reduce | flops 1 | bytes 8 | tf_op jit(solution)/shard_map/psum | solution.py:15
  198.1 9.2 %psum.58 = f32[]{:T(128)} all-reduce(f32[]{:T(128)} %psum.57), channel_id=1, replica_groups=mesh['chip_0'=4,'chip_1'=4,'chip_2'=2,'cores'=4] {'chip_2'}, use_global_device_ids=true, to_apply=%region_29.30 | all-reduce | flops 1 | bytes 8 | tf_op jit(solution)/shard_map/psum | solution.py:15
  207.3 5.3 %psum.61 = s32[]{:T(128)} all-reduce(s32[]{:T(128)} %psum.60), channel_id=1, replica_groups=mesh['chip_0'=4,'chip_1'=4,'chip_2'=2,'cores'=4] {'chip_1'}, use_global_device_ids=true, to_apply=%region_33.34 | all-reduce | flops 1 | bytes 8 | tf_op jit(solution)/shard_map/psum | solution.py:15
  214.0 8.6 %all-to-all-start = ((s32[32,1,1]{2,1,0:T(1,128)}), s32[32,1,1]{2,1,0:T(1,128)S(1)}, u32[]{:S(2)}, u32[]{:S(2)}) async-start(s32[32,1,1]{2,1,0:T(1,128)} %copy.43), calls=%async_computation | async-start | bytes 32768 | tf_op jit(solution)/shard_map/all_to_all | solution.py:125
  222.6 9.7 %psum.59 = f32[]{:T(128)} all-reduce(f32[]{:T(128)} %psum.58), channel_id=1, replica_groups=mesh['chip_0'=4,'chip_1'=4,'chip_2'=2,'cores'=4] {'cores'}, use_global_device_ids=true, to_apply=%region_30.31 | all-reduce | flops 1 | bytes 8 | tf_op jit(solution)/shard_map/psum | solution.py:15
  232.3 4.1 %psum.62 = s32[]{:T(128)} all-reduce(s32[]{:T(128)} %psum.61), channel_id=1, replica_groups=mesh['chip_0'=4,'chip_1'=4,'chip_2'=2,'cores'=4] {'chip_2'}, use_global_device_ids=true, to_apply=%region_34.35 | all-reduce | flops 1 | bytes 8 | tf_op jit(solution)/shard_map/psum | solution.py:15
  237.1 5.4 %psum.63 = s32[]{:T(128)} all-reduce(s32[]{:T(128)} %psum.62), channel_id=1, replica_groups=mesh['chip_0'=4,'chip_1'=4,'chip_2'=2,'cores'=4] {'cores'}, use_global_device_ids=true, to_apply=%region_35.36 | all-reduce | flops 1 | bytes 8 | tf_op jit(solution)/shard_map/psum | solution.py:15
  245.2 9.5 %all-to-all-start.1 = ((f32[32,1,512]{2,1,0:T(1,128)}), f32[32,1,512]{2,1,0:T(1,128)S(1)}, u32[]{:S(2)}, u32[]{:S(2)}) async-start(f32[32,1,512]{2,1,0:T(1,128)} %copy.44), calls=%async_computation.1 | async-start | bytes 131072 | tf_op jit(solution)/shard_map/all_to_all | solution.py:114
  255.3 6.7 %all-to-all-done.1 = f32[32,1,512]{2,1,0:T(1,128)S(1)} async-done(((f32[32,1,512]{2,1,0:T(1,128)}), f32[32,1,512]{2,1,0:T(1,128)S(1)}, u32[]{:S(2)}, u32[]{:S(2)}) %all-to-all-start.1) | async-done | bytes 65568 | tf_op jit(solution)/shard_map/all_to_all | solution.py:114
  262.0 1.3 scatter_custom_fusion.7
  (138 shorter events, 33.3 us)
Async XLA Ops:
  7.6 92.1 %copy-start.1 = (s32[32]{0:T(128)S(1)}, s32[32]{0:T(128)}, u32[]{:S(2)}) copy-start(s32[32]{0:T(128)} %param.17) | copy-start | bytes 388
  7.6 92.1 %copy-start.2 = (s32[32]{0:T(128)S(1)}, s32[32]{0:T(128)}, u32[]{:S(2)}) copy-start(s32[32]{0:T(128)} %param.18) | copy-start | bytes 388
  7.6 92.1 %copy-start.3 = (s32[32]{0:T(128)S(1)}, s32[32]{0:T(128)}, u32[]{:S(2)}) copy-start(s32[32]{0:T(128)} %param.19) | copy-start | bytes 388
  7.6 97.6 %copy-start = (f32[32,512]{1,0:T(8,128)S(1)}, f32[32,512]{1,0:T(8,128)}, u32[]{:S(2)}) copy-start(f32[32,512]{1,0:T(8,128)} %param.14) | copy-start | bytes 196612
  214.0 31.1 %all-to-all-start = ((s32[32,1,1]{2,1,0:T(1,128)}), s32[32,1,1]{2,1,0:T(1,128)S(1)}, u32[]{:S(2)}, u32[]{:S(2)}) async-start(s32[32,1,1]{2,1,0:T(1,128)} %copy.43), calls=%async_computation | async-start | bytes 32768 | tf_op jit(solution)/shard_map/all_to_all | solution.py:125
  245.2 16.9 %all-to-all-start.1 = ((f32[32,1,512]{2,1,0:T(1,128)}), f32[32,1,512]{2,1,0:T(1,128)S(1)}, u32[]{:S(2)}, u32[]{:S(2)}) async-start(f32[32,1,512]{2,1,0:T(1,128)} %copy.44), calls=%async_computation.1 | async-start | bytes 131072 | tf_op jit(solution)/shard_map/all_to_all | solution.py:114
where the time goes:
time: 265 us; the launch traced here: 264 us
  matrix products  85.6 us (32%)
  other arithmetic  77.7 us (29%)
  blocking collectives  59.4 us (22%)
  starting transfers between devices  18.1 us (7%)
  local copies, waits for them, and re-layouts  12.5 us (5%)
  waiting for transfers between devices  6.7 us (3%)
  between operations  3.34 us (1%)
    dot_general x9, matrix products, shock_table(): jnp.einsum('kj,kr->jr', features * coef_scale[:, None], market_draws, pre...  85.6 us
    psum x8, blocking collectives, by_axis(): return functools.reduce(lax.psum, axes, x)  59.4 us
    reduce_sum x28, other arithmetic, contract(): predicted = jnp.mean(utility / (1.0 + inside)[None, :], axis=1)  50 us
    reduce_sum x19, other arithmetic, contract(): inside = jnp.sum(utility, axis=0)  19.2 us
    all_to_all x1, starting transfers between devices, local(): lax.all_to_all(placed.reshape((chip_count, pair_room) + final_home.shape[...  9.51 us
    all_to_all x1, starting transfers between devices, local(): lax.all_to_all(slot_ids, CHIP, split_axis=0, concat_axis=0, tiled=True)  8.57 us
    all_to_all x1, waiting for transfers between devices, local(): lax.all_to_all(placed.reshape((chip_count, pair_room) + final_home.shape[...  6.7 us
  transfers between devices with their start and end apart: 2, of which 1 were waited for; matrix products, arithmetic and copies ran while one was open for 1% of the time, Pallas kernels for 0%

commit v1 on v0

v1 whole, which is shorter than its diff:
```python
import functools
import math

import jax
import jax.numpy as jnp
from jax import lax
from jax.experimental import pallas as pl
from jax.experimental.pallas import tpu as pltpu
from jax.sharding import Mesh
from jax.sharding import PartitionSpec as P

TAIL_ITERS = 4
CHIP = ("chip_0", "chip_1", "chip_2")
CHIP_CORES = ("chip_0", "chip_1", "chip_2", "cores")

GROUP = 4
LANES = 128
LOG2E = math.log2(math.e)
LIFT = 2.0**40
BF = jnp.bfloat16
F32 = jnp.float32


def three_parts(x):
    hi = x.astype(BF).astype(F32)
    mid = (x - hi).astype(BF).astype(F32)
    return hi, mid, x - hi - mid


def hi_lo_rows(x):
    hi = x.astype(BF).astype(F32)
    row = lax.broadcasted_iota(jnp.int32, x.shape, 0)
    return jnp.where(row % 2 == 0, hi, x - hi).astype(BF)


def add_pair(y):
    return y + pltpu.roll(y, 1, 0)


def dot(a, b):
    return jnp.dot(a, b, preferred_element_type=F32)


def markets_kernel(
    sigma, counts, converged, destination, start, chars, share, draws,
    delta, send,
    order, bucket_at, a_stack, b_stack, table, table_t, log_obs, goal, first, q_two, q_last,
    *, slots, cores,
):
    total, width = start.shape
    people = draws.shape[2]
    k_count = chars.shape[1]
    tiles = width // LANES
    scale = LIFT * people

    def bucket(i):
        return converged[i] * tiles + (tiles - (counts[i] + LANES - 1) // LANES)

    for b in range(2 * tiles):
        bucket_at[b] = 0

    def tally(i, _):
        b = bucket(i)
        bucket_at[b] = bucket_at[b] + 1
        return 0

    lax.fori_loop(0, total, tally, 0)
    at = jnp.int32(0)
    for b in range(2 * tiles):
        size = bucket_at[b]
        bucket_at[b] = at
        at = at + size

    def put(i, _):
        b = bucket(i)
        order[bucket_at[b]] = i
        bucket_at[b] = bucket_at[b] + 1
        return 0

    lax.fori_loop(0, total, put, 0)

    row8 = lax.broadcasted_iota(jnp.int32, (8, width), 0)
    lane = lax.broadcasted_iota(jnp.int32, (8, width), 1)
    lives = []
    for base in range(0, total, 8):
        count = jnp.zeros((8, width), jnp.int32)
        for i in range(8):
            count = jnp.where(row8 == i, counts[base + i], count)
        live = lane < count
        lives.append(live)
        rows = pl.ds(base, 8)
        obs = share[rows, :] - jnp.log(count.astype(F32)) - 1.5
        log_obs[rows, :] = obs
        wanted = jnp.where(live, jnp.exp(obs) * scale, 0.0)
        opening = jnp.where(live, jnp.exp(obs + start[rows, :]), 0.0)
        for i in range(8):
            goal[base + i] = jnp.broadcast_to(wanted[i : i + 1], (8, width))
            first[base + i] = jnp.broadcast_to(opening[i : i + 1], (8, width))

    a_stack[...] = jnp.zeros(a_stack.shape, F32)
    b_stack[...] = jnp.zeros(b_stack.shape, F32)
    kw = lax.broadcasted_iota(jnp.int32, (k_count, width), 0)
    coef = jnp.zeros((k_count, width), F32)
    for k in range(k_count):
        coef = jnp.where(kw == k, sigma[k] * LOG2E, coef)

    def put_stack(ref, parts):
        for i, part in enumerate(parts):
            ref[8 * i : 8 * i + k_count, :] = part

    def build(n, market, g):
        a1, a2, a3 = three_parts(chars[market] * coef)
        b1, b2, b3 = three_parts(draws[market])
        put_stack(a_stack, (a1, a1, a2, a1, a2, a3))
        put_stack(b_stack, (b1, b2, b1, b3, b2, b1))
        a = a_stack[:, :n]
        b = b_stack[...]
        a_t = jnp.transpose(a, (1, 0)).astype(BF)
        b_t = jnp.transpose(b, (1, 0)).astype(BF)
        table[g, :n, :] = jnp.exp2(dot(a_t, b.astype(BF))).astype(BF)
        table_t[g, :, :n] = jnp.exp2(dot(b_t, a.astype(BF))).astype(BF)

    def run_group(n, base):
        ids = [order[base + g] for g in range(GROUP)]
        busy = [1 - converged[i] for i in ids]
        iters = 2 + TAIL_ITERS * functools.reduce(jnp.maximum, busy)

        def build_one(g, _):
            build(n, order[base + g], g)
            return 0

        lax.fori_loop(0, GROUP, build_one, 0)
        goals = [goal[i, :, :n] for i in ids]
        firsts = [first[i, :, :n] for i in ids]

        def step(it, carry):
            insides = [add_pair(dot(hi_lo_rows(carry[g]), table[g, :n, :])) for g in range(GROUP)]
            weights = [hi_lo_rows(LIFT / (1.0 + x)) for x in insides]
            out = []
            for g in range(GROUP):
                q = add_pair(dot(weights[g], table_t[g, :, :n]))
                q_two[jnp.where(it == 1, ids[g], total), :, :n] = q
                keep = jnp.logical_or(it < 2, busy[g] == 1)
                q_last[jnp.where(keep, ids[g], total), :, :n] = q
                out.append(goals[g] / q)
            return tuple(out)

        lax.fori_loop(0, iters, step, tuple(firsts))

    def one_group(j, _):
        base = j * GROUP
        size = counts[order[base]]
        for g in range(1, GROUP):
            size = jnp.maximum(size, counts[order[base + g]])
        for t in range(1, tiles + 1):

            @pl.when((size + LANES - 1) // LANES == t)
            def _():
                run_group(t * LANES, base)

        return 0

    lax.fori_loop(0, total // GROUP, one_group, 0)

    side = lax.broadcasted_iota(jnp.int32, (1, LANES), 1)
    empty = jnp.where(side == 0, float(slots), 0.0)
    for c in range(send.shape[0]):
        send[c, :, width:] = empty
    acc = jnp.zeros((8, width), F32)
    for base in range(0, total, 8):
        rows = pl.ds(base, 8)
        obs = log_obs[rows, :] + math.log(scale)
        live = lives[base // 8]
        two = q_two[base]
        last = q_last[base]
        for i in range(1, 8):
            two = jnp.where(row8 == i, q_two[base + i], two)
            last = jnp.where(row8 == i, q_last[base + i], last)
        two = jnp.where(live, obs - jnp.log(two), 0.0)
        last = jnp.where(live, obs - jnp.log(last), 0.0)
        delta[rows, :] = last
        acc = acc + (last - two) * (last - two)
        for i in range(8):

            @pl.when(converged[base + i] == 0)
            def _():
                place = destination[base + i]
                chip = place // (slots * cores)
                send[chip, :, :width] = last[i : i + 1]
                slot = (place % slots).astype(F32)
                send[chip, :, width:] = jnp.where(side == 0, slot, 0.0)

    def tally_active(i, n):
        return n + jnp.where(converged[i] == 0, counts[i], 0)

    active = lax.fori_loop(0, total, tally_active, jnp.int32(0)).astype(F32)
    change = jnp.sum(jnp.sum(acc, axis=1, keepdims=True), axis=0, keepdims=True)
    for c in range(send.shape[0]):
        row = send[c, :, width:]
        row = jnp.where(side == 1, change, row)
        send[c, :, width:] = jnp.where(side == 2, active, row)


def same_order_sum(x, axis):
    size = lax.axis_size(axis)
    here = lax.axis_index(axis)
    parts = [x] + [
        lax.ppermute(x, axis, [(i, (i + k) % size) for i in range(size)]) for k in range(1, size)
    ]
    total = 0.0
    for source in range(size):
        for k, part in enumerate(parts):
            total = total + jnp.where((here - k) % size == source, part, 0.0)
    return total


def local(start_offset, chars, share_rel, draws, sigma, counts, converged, destination):
    market_count, width = start_offset.shape
    k_count, people = draws.shape[1:]
    chip_count = lax.axis_size(CHIP)
    cores = lax.axis_size("cores")
    slots = 3 * market_count // 8
    smem = pl.BlockSpec(memory_space=pltpu.SMEM)
    vmem = pl.BlockSpec(memory_space=pltpu.VMEM)
    delta, send = pl.pallas_call(
        functools.partial(markets_kernel, slots=slots, cores=cores),
        out_shape=(
            jax.ShapeDtypeStruct((market_count, width), F32),
            jax.ShapeDtypeStruct((chip_count, 1, width + LANES), F32),
        ),
        in_specs=[smem] * 4 + [vmem] * 4,
        out_specs=(vmem,) * 2,
        scratch_shapes=[
            pltpu.SMEM((market_count,), jnp.int32),
            pltpu.SMEM((2 * width // LANES,), jnp.int32),
            pltpu.VMEM((48, width), F32),
            pltpu.VMEM((48, people), F32),
            pltpu.VMEM((GROUP, width, people), BF),
            pltpu.VMEM((GROUP, people, width), BF),
            pltpu.VMEM((market_count, width), F32),
            pltpu.VMEM((market_count, 8, width), F32),
            pltpu.VMEM((market_count, 8, width), F32),
            pltpu.VMEM((market_count + 1, 8, width), F32),
            pltpu.VMEM((market_count + 1, 8, width), F32),
        ],
        compiler_params=pltpu.CompilerParams(vmem_limit_bytes=48 * 2**20),
        name="markets",
    )(sigma, counts, converged, destination, start_offset, chars, share_rel, draws)

    values = lax.all_to_all(send, CHIP, split_axis=0, concat_axis=0, tiled=True)
    values = values.reshape(chip_count, width + LANES)
    named = jnp.arange(slots, dtype=F32)[:, None, None] == values[None, :, width : width + 1]
    work_delta = jnp.sum(jnp.where(named, values[None, :, :width], 0.0), axis=1)
    totals = same_order_sum(jnp.sum(values[:, width + 1 : width + 3], axis=0), "cores")
    return delta, work_delta, jnp.sqrt(totals[0] / totals[1])


def solution(mesh):
    finer = Mesh(
        mesh.devices.reshape(4, 4, 2, mesh.shape["cores"]), ("chip_0", "chip_1", "chip_2", "cores")
    )
    row = P(CHIP_CORES)
    return jax.shard_map(
        local,
        mesh=finer,
        in_specs=(row, row, row, row, P(), row, row, row),
        out_specs=(row, row, P()),
        check_vma=False,
    )
```

time: 265 us -> 81.5 us (0.31)
  the two profiles are of different devices: /device:TPU:1 before, /device:TPU:0 now
where the time goes in v1:
time: 81.5 us; the launch traced here: 80.2 us
  Pallas kernels  34.5 us (42%)
  starting transfers between devices  30.5 us (37%)
  waiting for transfers between devices  8.26 us (10%)
  between operations  3.24 us (4%)
  local copies, waits for them, and re-layouts  2.84 us (3%)
  other arithmetic  0.91 us (1%)
    pallas_call x1, Pallas kernels, local(): pl.pallas_call(functools.partial(markets_kernel, slots=slots, cores=cores...  34.5 us
    all_to_all x1, starting transfers between devices, local(): values = lax.all_to_all(send, CHIP, split_axis=0, concat_axis=0, tiled=True)  26.4 us
    all_to_all x1, waiting for transfers between devices, local(): values = lax.all_to_all(send, CHIP, split_axis=0, concat_axis=0, tiled=True)  7.48 us
    ppermute x3, starting transfers between devices, same_order_sum(): lax.ppermute(x, axis, [(i, (i + k) % size) for i in range(size)])  4.1 us
    unnamed x17, local copies, waits for them, and re-layouts  2.14 us
  transfers between devices with their start and end apart: 4, of which 3 were waited for; matrix products, arithmetic and copies ran while one was open for 1% of the time, Pallas kernels for 0%

profile of v1, /device:TPU:0, one launch (start us, length us, event | category | flops | bytes accessed | tf_op | source)
XLA Modules:
  0.0 80.2 jit_solution(7636255611581102185)
XLA Ops:
  0.6 0.0 copy-start.6
  0.6 1.3 %copy.15.chars = f32[32,6,512]{2,1,0:T(8,128)S(1)} copy(f32[32,6,512]{2,0,1:T(8,128)} %param.9) | data formatting | bytes 786432 | tf_op args[1]
  1.9 0.0 copy-done.6
  1.9 0.0 copy-start
  2.0 0.0 copy-start.1
  2.0 0.0 copy-start.2
  2.0 0.0 copy-start.3
  2.0 0.0 copy-start.4
  2.0 0.0 copy-start.5
  2.0 0.4 copy.16.draws
  2.4 0.4 copy-done
  2.8 0.0 copy-done.1
  2.8 0.0 copy-done.2
  2.8 0.0 copy-done.3
  2.8 0.0 copy-done.4
  2.8 0.0 copy-done.5
  2.8 34.5 %markets.1 = (f32[32,512]{1,0:T(8,128)}, f32[32,1,640]{2,1,0:T(1,128)}) custom-call(f32[6]{0:T(128)S(1)} %copy-done.2, s32[32]{0:T(128)S(1)} %copy-done.3, s32[32]{0:T(128)S(1)} %copy-done.4, s32[32]{0:T(128)S(1)} %copy-done.5, f32[32,512]{1,0:T(8,128)S(1)} %copy-done, f32[32,6,512]{2,1,0:T(8,128)S(1)} %copy.15.chars, f32[32,512]{1,0:T(8,128)S(1)} %copy-done.1, ...), custom_call_target="tpu_custom_call" | custom-call | tf_op jit(solution)/shard_map/markets/pallas_call | solution.py:225
  37.4 26.4 %all-to-all-start = ((f32[32,1,640]{2,1,0:T(1,128)}), f32[32,1,640]{2,1,0:T(1,128)S(1)}, u32[]{:S(2)}, u32[]{:S(2)}) async-start(f32[32,1,640]{2,1,0:T(1,128)} %get-tuple-element.6), calls=%async_computation | async-start | bytes 163840 | tf_op jit(solution)/shard_map/all_to_all | solution.py:250
  63.8 7.5 %all-to-all-done = f32[32,1,640]{2,1,0:T(1,128)S(1)} async-done(((f32[32,1,640]{2,1,0:T(1,128)}), f32[32,1,640]{2,1,0:T(1,128)S(1)}, u32[]{:S(2)}, u32[]{:S(2)}) %all-to-all-start) | async-done | bytes 81952 | tf_op jit(solution)/shard_map/all_to_all | solution.py:250
  71.3 0.1 slice_reduce_fusion.1
  71.4 0.1 slice_reduce_fusion
  71.5 0.1 collective-permute-start
  71.6 1.5 %collective-permute-start.1 = (f32[2]{0:T(128)S(1)}, f32[2]{0:T(128)S(1)}, u32[]{:S(2)}, u32[]{:S(2)}) collective-permute-start(f32[2]{0:T(128)S(1)} %slice_reduce_fusion), channel_id=1, source_target_pairs={{0,2},{1,3},{2,0},{3,1},{4,6},{5,7},{6,4},{7,5},{8,10},{9,11},{10,... | collective-permute-start | bytes 32 | tf_op jit(solution)/shard_map/ppermute | solution.py:208
  73.1 2.5 %collective-permute-start.2 = (f32[2]{0:T(128)S(1)}, f32[2]{0:T(128)S(1)}, u32[]{:S(2)}, u32[]{:S(2)}) collective-permute-start(f32[2]{0:T(128)S(1)} %slice_reduce_fusion), channel_id=1, source_target_pairs={{0,3},{1,0},{2,1},{3,2},{4,7},{5,4},{6,5},{7,6},{8,11},{9,8},{10,9... | collective-permute-start | bytes 32 | tf_op jit(solution)/shard_map/ppermute | solution.py:208
  75.6 0.8 select_reduce_fusion
  76.4 0.0 collective-permute-done
  76.4 0.3 collective-permute-done.1
  76.7 0.5 collective-permute-done.2
  77.2 0.6 fusion.15
  (4 shorter events, 0.0 us)
Async XLA Ops:
  0.6 1.3 %copy-start.6 = (f32[32,6,768]{2,0,1:T(8,128)S(1)}, f32[32,6,768]{2,0,1:T(8,128)}, u32[]{:S(2)}) copy-start(f32[32,6,768]{2,0,1:T(8,128)} %param.11) | copy-start | bytes 1769476
  1.9 0.8 %copy-start = (f32[32,512]{1,0:T(8,128)S(1)}, f32[32,512]{1,0:T(8,128)}, u32[]{:S(2)}) copy-start(f32[32,512]{1,0:T(8,128)} %start.1) | copy-start | bytes 196612
  2.0 0.9 %copy-start.1 = (f32[32,512]{1,0:T(8,128)S(1)}, f32[32,512]{1,0:T(8,128)}, u32[]{:S(2)}) copy-start(f32[32,512]{1,0:T(8,128)} %share.1) | copy-start | bytes 196612
  2.0 0.9 %copy-start.2 = (f32[6]{0:T(128)S(1)}, f32[6]{0:T(128)}, u32[]{:S(2)}) copy-start(f32[6]{0:T(128)} %sigma.1) | copy-start | bytes 76
  2.0 0.8 %copy-start.3 = (s32[32]{0:T(128)S(1)}, s32[32]{0:T(128)}, u32[]{:S(2)}) copy-start(s32[32]{0:T(128)} %counts.1) | copy-start | bytes 388
  2.0 0.8 %copy-start.4 = (s32[32]{0:T(128)S(1)}, s32[32]{0:T(128)}, u32[]{:S(2)}) copy-start(s32[32]{0:T(128)} %converged.1) | copy-start | bytes 388
  2.0 0.8 %copy-start.5 = (s32[32]{0:T(128)S(1)}, s32[32]{0:T(128)}, u32[]{:S(2)}) copy-start(s32[32]{0:T(128)} %destination.1) | copy-start | bytes 388
  37.4 33.9 %all-to-all-start = ((f32[32,1,640]{2,1,0:T(1,128)}), f32[32,1,640]{2,1,0:T(1,128)S(1)}, u32[]{:S(2)}, u32[]{:S(2)}) async-start(f32[32,1,640]{2,1,0:T(1,128)} %get-tuple-element.6), calls=%async_computation | async-start | bytes 163840 | tf_op jit(solution)/shard_map/all_to_all | solution.py:250
  71.5 4.9 %collective-permute-start = (f32[2]{0:T(128)S(1)}, f32[2]{0:T(128)S(1)}, u32[]{:S(2)}, u32[]{:S(2)}) collective-permute-start(f32[2]{0:T(128)S(1)} %slice_reduce_fusion), channel_id=1, source_target_pairs={{0,1},{1,2},{2,3},{3,0},{4,5},{5,6},{6,7},{7,4},{8,9},{9,10},{10,1... | collective-permute-start | bytes 32 | tf_op jit(solution)/shard_map/ppermute | solution.py:208
  71.6 5.2 %collective-permute-start.1 = (f32[2]{0:T(128)S(1)}, f32[2]{0:T(128)S(1)}, u32[]{:S(2)}, u32[]{:S(2)}) collective-permute-start(f32[2]{0:T(128)S(1)} %slice_reduce_fusion), channel_id=1, source_target_pairs={{0,2},{1,3},{2,0},{3,1},{4,6},{5,7},{6,4},{7,5},{8,10},{9,11},{10,... | collective-permute-start | bytes 32 | tf_op jit(solution)/shard_map/ppermute | solution.py:208
  73.1 4.1 %collective-permute-start.2 = (f32[2]{0:T(128)S(1)}, f32[2]{0:T(128)S(1)}, u32[]{:S(2)}, u32[]{:S(2)}) collective-permute-start(f32[2]{0:T(128)S(1)} %slice_reduce_fusion), channel_id=1, source_target_pairs={{0,3},{1,0},{2,1},{3,2},{4,7},{5,4},{6,5},{7,6},{8,11},{9,8},{10,9... | collective-permute-start | bytes 32 | tf_op jit(solution)/shard_map/ppermute | solution.py:208

commit v2 on v1

v2 whole, which is shorter than its diff:
```python
import functools
import math

import jax
import jax.numpy as jnp
from jax import lax
from jax.experimental import pallas as pl
from jax.experimental.pallas import tpu as pltpu
from jax.sharding import Mesh
from jax.sharding import PartitionSpec as P

TAIL_ITERS = 4
CHIP_CORES = ("chip_0", "chip_1", "chip_2", "cores")

GROUP = 4
EARLY = 20
LANES = 128
LOG2E = math.log2(math.e)
LIFT = 2.0**40
BF = jnp.bfloat16
F32 = jnp.float32


def three_parts(x):
    hi = x.astype(BF).astype(F32)
    mid = (x - hi).astype(BF).astype(F32)
    return hi, mid, x - hi - mid


def hi_lo_rows(x):
    hi = x.astype(BF).astype(F32)
    row = lax.broadcasted_iota(jnp.int32, x.shape, 0)
    return jnp.where(row < 4, hi, x - hi).astype(BF)


def add_halves(y):
    return y + pltpu.roll(y, 4, 0)


def by_turns(a, b):
    row = lax.broadcasted_iota(jnp.int32, a.shape, 0)
    return jnp.where(row % 2 == 0, a, b)


def dot(a, b):
    return jnp.dot(a, b, preferred_element_type=F32)


def sort_markets(counts, converged, order, bucket_at, total, tiles):
    def bucket(i):
        return converged[i] * tiles + (tiles - (counts[i] + LANES - 1) // LANES)

    for b in range(2 * tiles):
        bucket_at[b] = 0

    def tally(i, active):
        b = bucket(i)
        bucket_at[b] = bucket_at[b] + 1
        return active + jnp.where(converged[i] == 0, counts[i], 0)

    active = lax.fori_loop(0, total, tally, jnp.int32(0))
    at = jnp.int32(0)
    for b in range(2 * tiles):
        size = bucket_at[b]
        bucket_at[b] = at
        at = at + size

    def put(i, _):
        b = bucket(i)
        order[bucket_at[b]] = i
        bucket_at[b] = bucket_at[b] + 1
        return 0

    lax.fori_loop(0, total, put, 0)
    return active


def early_kernel(
    sigma, counts, converged, destination, start, chars, share, draws,
    delta, send, order,
    bucket_at, *scratch, slots,
):
    total, width = start.shape
    active = sort_markets(counts, converged, order, bucket_at, total, width // LANES)
    final_rows = run_markets(
        sigma, counts, converged, start, chars, share, draws, order, *scratch, 0, EARLY
    )
    row8 = lax.broadcasted_iota(jnp.int32, (8, width), 0)
    acc = jnp.zeros((8, width), F32)
    for base in range(0, total, 8):
        two, last = final_rows(base)
        delta[pl.ds(base, 8), :] = last
        done = jnp.ones((8, width), jnp.int32)
        for i in range(8):
            done = jnp.where(row8 == i, converged[base + i], done)
        step = jnp.where(done == 0, last - two, 0.0)
        acc = acc + step * step

    change = jnp.sum(jnp.sum(acc, axis=1, keepdims=True), axis=0, keepdims=True)
    side = lax.broadcasted_iota(jnp.int32, (1, LANES), 1)
    empty = jnp.where(side == 1, change, jnp.where(side == 2, active.astype(F32), float(slots)))
    for c in range(send.shape[0]):
        send[c, :, width:] = empty
    for i in range(total):

        @pl.when(converged[i] == 0)
        def _():
            device = destination[i] // slots
            slot = (destination[i] % slots).astype(F32)
            send[device, :, :width] = delta[i : i + 1, :]
            send[device, :, width:] = jnp.where(side == 0, slot, empty)


def late_kernel(
    sigma, counts, converged, order, start, chars, share, draws, early,
    delta,
    late, *scratch,
):
    total, width = start.shape
    final_rows = run_markets(
        sigma, counts, converged, start, chars, share, draws, order, *scratch, EARLY, total
    )
    for i in range(total):
        late[order[i]] = 1 if i >= EARLY else 0
    row8 = lax.broadcasted_iota(jnp.int32, (8, width), 0)
    for base in range(0, total, 8):
        rows = pl.ds(base, 8)
        here = jnp.zeros((8, width), jnp.int32)
        for i in range(8):
            here = jnp.where(row8 == i, late[base + i], here)
        delta[rows, :] = jnp.where(here == 1, final_rows(base)[1], early[rows, :])


def run_markets(
    sigma, counts, converged, start, chars, share, draws, order,
    a_stack, b_stack, table, table_t, log_obs, goal, first, q_two, q_last,
    begin, end,
):
    total, width = start.shape
    people = draws.shape[2]
    k_count = chars.shape[1]
    tiles = width // LANES
    scale = LIFT * people

    row8 = lax.broadcasted_iota(jnp.int32, (8, width), 0)
    lane = lax.broadcasted_iota(jnp.int32, (8, width), 1)
    lives = []
    for base in range(0, total, 8):
        count = jnp.zeros((8, width), jnp.int32)
        for i in range(8):
            count = jnp.where(row8 == i, counts[base + i], count)
        live = lane < count
        lives.append(live)
        rows = pl.ds(base, 8)
        obs = share[rows, :] - jnp.log(count.astype(F32)) - 1.5
        log_obs[rows, :] = obs
        wanted = jnp.where(live, jnp.exp(obs) * scale, 0.0)
        opening = jnp.where(live, jnp.exp(obs + start[rows, :]), 0.0)
        for i in range(8):
            goal[base + i] = jnp.broadcast_to(wanted[i : i + 1], (8, width))
            first[base + i] = jnp.broadcast_to(opening[i : i + 1], (8, width))

    a_stack[...] = jnp.zeros(a_stack.shape, F32)
    b_stack[...] = jnp.zeros(b_stack.shape, F32)
    kw = lax.broadcasted_iota(jnp.int32, (k_count, width), 0)
    coef = jnp.zeros((k_count, width), F32)
    for k in range(k_count):
        coef = jnp.where(kw == k, sigma[k] * LOG2E, coef)

    def put_stack(ref, g, parts):
        for i, part in enumerate(parts):
            ref[g, 8 * i : 8 * i + k_count, :] = part

    def build(n, market, g):
        a1, a2, a3 = three_parts(chars[market] * coef)
        b1, b2, b3 = three_parts(draws[market])
        put_stack(a_stack, g, (a1, a1, a2, a1, a2, a3))
        put_stack(b_stack, g, (b1, b2, b1, b3, b2, b1))
        a_t = jnp.transpose(a_stack[g, :, :n], (1, 0)).astype(BF)
        t = jnp.exp2(dot(a_t, b_stack[g].astype(BF))).astype(BF)
        table[g, :n, :] = t
        at = (g % 2) * n
        table_t[g // 2, :, at : at + n] = jnp.transpose(t, (1, 0))

    def run_group(n, base):
        ids = [order[base + g] for g in range(GROUP)]
        busy = [1 - converged[i] for i in ids]
        iters = 2 + TAIL_ITERS * functools.reduce(jnp.maximum, busy)
        for g in range(GROUP):
            build(n, ids[g], g)
        pairs = range(GROUP // 2)
        goals = [by_turns(goal[ids[2 * p], :, :n], goal[ids[2 * p + 1], :, :n]) for p in pairs]
        firsts = [by_turns(first[ids[2 * p], :, :n], first[ids[2 * p + 1], :, :n]) for p in pairs]

        def step(it, carry):
            weights = []
            for p in pairs:
                e = hi_lo_rows(carry[p])
                inside = by_turns(dot(e, table[2 * p, :n, :]), dot(e, table[2 * p + 1, :n, :]))
                weights.append(hi_lo_rows(LIFT / (1.0 + add_halves(inside))))
            out = []
            for p in pairs:
                y = dot(weights[p], table_t[p, :, : 2 * n])
                q = add_halves(by_turns(y[:, :n], y[:, n:]))
                other = pltpu.roll(q, 1, 0)
                for g, rows in ((2 * p, by_turns(q, other)), (2 * p + 1, by_turns(other, q))):
                    q_two[jnp.where(it == 1, ids[g], total), :, :n] = rows
                    keep = jnp.logical_or(it < 2, busy[g] == 1)
                    q_last[jnp.where(keep, ids[g], total), :, :n] = rows
                out.append(goals[p] / q)
            return tuple(out)

        lax.fori_loop(0, iters, step, tuple(firsts))

    def one_group(j, _):
        base = j * GROUP
        size = counts[order[base]]
        for g in range(1, GROUP):
            size = jnp.maximum(size, counts[order[base + g]])
        for t in range(1, tiles + 1):

            @pl.when((size + LANES - 1) // LANES == t)
            def _():
                run_group(t * LANES, base)

        return 0

    lax.fori_loop(begin // GROUP, end // GROUP, one_group, 0)

    def final_rows(base):
        obs = log_obs[pl.ds(base, 8), :] + math.log(scale)
        live = lives[base // 8]
        two = q_two[base]
        last = q_last[base]
        for i in range(1, 8):
            two = jnp.where(row8 == i, q_two[base + i], two)
            last = jnp.where(row8 == i, q_last[base + i], last)
        return (
            jnp.where(live, obs - jnp.log(two), 0.0),
            jnp.where(live, obs - jnp.log(last), 0.0),
        )

    return final_rows


def scratch_for(total, width, people):
    return [
        pltpu.VMEM((GROUP, 48, width), F32),
        pltpu.VMEM((GROUP, 48, people), F32),
        pltpu.VMEM((GROUP, width, people), BF),
        pltpu.VMEM((GROUP // 2, people, 2 * width), BF),
        pltpu.VMEM((total, width), F32),
        pltpu.VMEM((total, 8, width), F32),
        pltpu.VMEM((total, 8, width), F32),
        pltpu.VMEM((total + 1, 8, width), F32),
        pltpu.VMEM((total + 1, 8, width), F32),
    ]


def early_markets(
    sigma, counts, converged, destination, start_offset, chars, share_rel, draws,
    *, devices, slots,
):
    total, width = start_offset.shape
    people = draws.shape[2]
    smem = pl.BlockSpec(memory_space=pltpu.SMEM)
    vmem = pl.BlockSpec(memory_space=pltpu.VMEM)
    return pl.pallas_call(
        functools.partial(early_kernel, slots=slots),
        out_shape=(
            jax.ShapeDtypeStruct((total, width), F32),
            jax.ShapeDtypeStruct((devices, 1, width + LANES), F32),
            jax.ShapeDtypeStruct((total,), jnp.int32),
        ),
        in_specs=[smem] * 4 + [vmem] * 4,
        out_specs=(vmem, vmem, smem),
        scratch_shapes=[pltpu.SMEM((2 * width // LANES,), jnp.int32)]
        + scratch_for(total, width, people),
        compiler_params=pltpu.CompilerParams(vmem_limit_bytes=48 * 2**20),
        name="early_markets",
    )(sigma, counts, converged, destination, start_offset, chars, share_rel, draws)


def late_markets(
    sigma, counts, converged, order, start_offset, chars, share_rel, draws, early
):
    total, width = start_offset.shape
    people = draws.shape[2]
    smem = pl.BlockSpec(memory_space=pltpu.SMEM)
    vmem = pl.BlockSpec(memory_space=pltpu.VMEM)
    rest = total - EARLY
    return pl.pallas_call(
        late_kernel,
        out_shape=jax.ShapeDtypeStruct((total, width), F32),
        in_specs=[smem] * 4 + [vmem] * 5,
        out_specs=vmem,
        scratch_shapes=[pltpu.SMEM((total,), jnp.int32)] + scratch_for(total, width, people),
        input_output_aliases={8: 0},
        compiler_params=pltpu.CompilerParams(vmem_limit_bytes=48 * 2**20),
        cost_estimate=pl.CostEstimate(
            flops=rest * width * people * 20,
            bytes_accessed=2 * 2**20,
            transcendentals=rest * width * people,
        ),
        name="late_markets",
    )(sigma, counts, converged, order, start_offset, chars, share_rel, draws, early)


def local(start_offset, chars, share_rel, draws, sigma, counts, converged, destination):
    market_count, width = start_offset.shape
    devices = lax.axis_size(CHIP_CORES)
    slots = 3 * market_count // 8
    early, send, order = early_markets(
        sigma, counts, converged, destination, start_offset, chars, share_rel, draws,
        devices=devices, slots=slots,
    )
    values = lax.all_to_all(send, CHIP_CORES, split_axis=0, concat_axis=0, tiled=True)
    delta = late_markets(
        sigma, counts, converged, order, start_offset, chars, share_rel, draws, early
    )
    values = values.reshape(devices, width + LANES)
    named = jnp.arange(slots, dtype=F32)[:, None, None] == values[None, :, width : width + 1]
    work_delta = jnp.sum(jnp.where(named, values[None, :, :width], 0.0), axis=1)
    totals = jnp.sum(values[:, width + 1 : width + 3], axis=0)
    return delta, work_delta, jnp.sqrt(totals[0] / totals[1])


def solution(mesh):
    finer = Mesh(
        mesh.devices.reshape(4, 4, 2, mesh.shape["cores"]), ("chip_0", "chip_1", "chip_2", "cores")
    )
    row = P(CHIP_CORES)
    return jax.shard_map(
        local,
        mesh=finer,
        in_specs=(row, row, row, row, P(), row, row, row),
        out_specs=(row, row, P()),
        check_vma=False,
    )
```

time: 81.5 us -> 65.4 us (0.80)
  the two profiles are of different devices: /device:TPU:0 before, /device:TPU:1 now
where the time goes in v2:
time: 65.4 us; the launch traced here: 64.6 us
  Pallas kernels  30 us (46%)
  starting transfers between devices  23.1 us (35%)
  waiting for transfers between devices  4.31 us (7%)
  between operations  3.26 us (5%)
  local copies, waits for them, and re-layouts  2.88 us (4%)
  other arithmetic  1.08 us (2%)
    all_to_all x1, starting transfers between devices, local(): lax.all_to_all(send, CHIP_CORES, split_axis=0, concat_axis=0, tiled=True)  23.1 us
    pallas_call x1, Pallas kernels, early_markets(): pl.pallas_call(functools.partial(early_kernel, slots=slots), out_shape=(j...  22.3 us
    pallas_call x1, Pallas kernels, late_markets(): pl.pallas_call(late_kernel, out_shape=jax.ShapeDtypeStruct((total, width)...  7.69 us
    all_to_all x1, waiting for transfers between devices, local(): lax.all_to_all(send, CHIP_CORES, split_axis=0, concat_axis=0, tiled=True)  4.31 us
    unnamed x17, local copies, waits for them, and re-layouts  2.15 us
  transfers between devices with their start and end apart: 1, of which 1 were waited for; matrix products, arithmetic and copies ran while one was open for 0% of the time, Pallas kernels for 12%

profile of v2, /device:TPU:1, one launch (start us, length us, event | category | flops | bytes accessed | tf_op | source)
XLA Modules:
  0.0 64.6 jit_solution(1855982924557820300)
XLA Ops:
  0.6 0.0 copy-start.6
  0.6 1.3 %copy.20.chars = f32[32,6,512]{2,1,0:T(8,128)S(1)} copy(f32[32,6,512]{2,0,1:T(8,128)} %param.9) | data formatting | bytes 786432 | tf_op args[1]
  1.9 0.0 copy-done.6
  1.9 0.0 copy-start
  2.0 0.0 copy-start.1
  2.0 0.0 copy-start.2
  2.0 0.0 copy-start.3
  2.0 0.0 copy-start.4
  2.0 0.0 copy-start.5
  2.0 0.4 copy.21.draws
  2.4 0.4 copy-done
  2.8 0.0 copy-done.1
  2.8 0.0 copy-done.2
  2.8 0.0 copy-done.3
  2.8 0.0 copy-done.4
  2.8 0.0 copy-done.5
  2.8 22.3 %early_markets.1 = (f32[32,512]{1,0:T(8,128)}, f32[128,1,640]{2,1,0:T(1,128)}, s32[32]{0:T(128)S(1)}) custom-call(f32[6]{0:T(128)S(1)} %copy-done.3, s32[32]{0:T(128)S(1)} %copy-done.4, s32[32]{0:T(128)S(1)} %copy-done.5, s32[32]{0:T(128)S(1)} %copy-done.2, f32[32,512]{1,0:T(8,128)S(1)} %copy-done, f32[32,6,512]{2,1,0:T(8,128)S(1)} %copy.20.chars, ...), custom_call_target="tpu_custom_call" | custom-call | tf_op jit(solution)/shard_map/early_markets/pallas_call | solution.py:268
  25.1 23.1 %all-to-all-start = ((f32[128,1,640]{2,1,0:T(1,128)}), f32[128,1,640]{2,1,0:T(1,128)S(1)}, u32[]{:S(2)}, u32[]{:S(2)}) async-start(f32[128,1,640]{2,1,0:T(1,128)} %get-tuple-element.8), calls=%async_computation | async-start | bytes 655360 | tf_op jit(solution)/shard_map/all_to_all | solution.py:317
  48.2 7.7 %late_markets.1 = f32[32,512]{1,0:T(8,128)} custom-call(f32[6]{0:T(128)S(1)} %copy-done.3, s32[32]{0:T(128)S(1)} %copy-done.4, s32[32]{0:T(128)S(1)} %copy-done.5, s32[32]{0:T(128)S(1)} %get-tuple-element.6.order, f32[32,512]{1,0:T(8,128)S(1)} %copy-done, f32[32,6,512]{2,1,0:T(8,128)S(1)} %copy.20.chars, ...), custom_call_target="tpu_custom_call", output_to_operand_aliasing={{}: (8, {})} | custom-call | flops 94371840 | bytes 2097152 | tf_op jit(solution)/shard_map/late_markets/pallas_call | solution.py:292
  55.9 4.3 %all-to-all-done = f32[128,1,640]{2,1,0:T(1,128)S(1)} async-done(((f32[128,1,640]{2,1,0:T(1,128)}), f32[128,1,640]{2,1,0:T(1,128)S(1)}, u32[]{:S(2)}, u32[]{:S(2)}) %all-to-all-start) | async-done | bytes 327712 | tf_op jit(solution)/shard_map/all_to_all | solution.py:317
  60.2 0.1 slice_reduce_fusion
  60.3 0.1 slice_reduce_fusion.1
  60.5 0.6 fusion
  62.5 1.0 %select_reduce_fusion = f32[12,512]{1,0:T(8,128)} fusion(f32[128,512]{1,0:T(8,128)S(1)} %slice.21, pred[12,128]{1,0:T(8,128)(4,1)S(1)} %iota_compare_fusion), kind=kLoop, calls=%fused_computation | loop fusion | flops 1566720 | bytes 288256 | tf_op jit(solution)/shard_map/reduce_sum | solution.py:323
  (3 shorter events, 0.1 us)
Async XLA Ops:
  0.6 1.3 %copy-start.6 = (f32[32,6,768]{2,0,1:T(8,128)S(1)}, f32[32,6,768]{2,0,1:T(8,128)}, u32[]{:S(2)}) copy-start(f32[32,6,768]{2,0,1:T(8,128)} %param.11) | copy-start | bytes 1769476
  1.9 0.8 %copy-start = (f32[32,512]{1,0:T(8,128)S(1)}, f32[32,512]{1,0:T(8,128)}, u32[]{:S(2)}) copy-start(f32[32,512]{1,0:T(8,128)} %start.3) | copy-start | bytes 196612
  2.0 0.9 %copy-start.1 = (f32[32,512]{1,0:T(8,128)S(1)}, f32[32,512]{1,0:T(8,128)}, u32[]{:S(2)}) copy-start(f32[32,512]{1,0:T(8,128)} %share.3) | copy-start | bytes 196612
  2.0 0.9 %copy-start.2 = (s32[32]{0:T(128)S(1)}, s32[32]{0:T(128)}, u32[]{:S(2)}) copy-start(s32[32]{0:T(128)} %destination.1) | copy-start | bytes 388
  2.0 0.8 %copy-start.3 = (f32[6]{0:T(128)S(1)}, f32[6]{0:T(128)}, u32[]{:S(2)}) copy-start(f32[6]{0:T(128)} %sigma.3) | copy-start | bytes 76
  2.0 0.8 %copy-start.4 = (s32[32]{0:T(128)S(1)}, s32[32]{0:T(128)}, u32[]{:S(2)}) copy-start(s32[32]{0:T(128)} %counts.3) | copy-start | bytes 388
  2.0 0.8 %copy-start.5 = (s32[32]{0:T(128)S(1)}, s32[32]{0:T(128)}, u32[]{:S(2)}) copy-start(s32[32]{0:T(128)} %converged.3) | copy-start | bytes 388
  25.1 35.1 %all-to-all-start = ((f32[128,1,640]{2,1,0:T(1,128)}), f32[128,1,640]{2,1,0:T(1,128)S(1)}, u32[]{:S(2)}, u32[]{:S(2)}) async-start(f32[128,1,640]{2,1,0:T(1,128)} %get-tuple-element.8), calls=%async_computation | async-start | bytes 655360 | tf_op jit(solution)/shard_map/all_to_all | solution.py:317

commit v3 on v2

--- a/solution.py
+++ b/solution.py
@@ -78,12 +78,26 @@
 def early_kernel(
     sigma, counts, converged, destination, start, chars, share, draws,
     delta, send, order,
-    bucket_at, *scratch, slots,
+    bucket_at, start_here, chars_here, share_here, draws_here, copied, *scratch, slots,
 ):
     total, width = start.shape
+    copies = [
+        pltpu.make_async_copy(source, here, copied.at[i])
+        for i, (source, here) in enumerate(
+            ((start, start_here), (share, share_here), (chars, chars_here), (draws, draws_here))
+        )
+    ]
+    for copy in copies:
+        copy.start()
+
+    def ready(which):
+        for copy in copies[which]:
+            copy.wait()
+
     active = sort_markets(counts, converged, order, bucket_at, total, width // LANES)
     final_rows = run_markets(
-        sigma, counts, converged, start, chars, share, draws, order, *scratch, 0, EARLY
+        sigma, counts, converged, start_here, chars_here, share_here, draws_here, order, *scratch,
+        0, EARLY, ready,
     )
     row8 = lax.broadcasted_iota(jnp.int32, (8, width), 0)
     acc = jnp.zeros((8, width), F32)
@@ -133,18 +147,19 @@
 
 def run_markets(
     sigma, counts, converged, start, chars, share, draws, order,
-    a_stack, b_stack, table, table_t, log_obs, goal, first, q_two, q_last,
-    begin, end,
+    chars_rows, draws_rows, a_stack, b_stack, table, table_t, log_obs, goal, first, q_two, q_last,
+    begin, end, ready=lambda which: None,
 ):
     total, width = start.shape
     people = draws.shape[2]
-    k_count = chars.shape[1]
+    k_count = chars.shape[0]
     tiles = width // LANES
     scale = LIFT * people
 
     row8 = lax.broadcasted_iota(jnp.int32, (8, width), 0)
     lane = lax.broadcasted_iota(jnp.int32, (8, width), 1)
     lives = []
+    ready(slice(0, 2))
     for base in range(0, total, 8):
         count = jnp.zeros((8, width), jnp.int32)
         for i in range(8):
@@ -160,20 +175,28 @@
             goal[base + i] = jnp.broadcast_to(wanted[i : i + 1], (8, width))
             first[base + i] = jnp.broadcast_to(opening[i : i + 1], (8, width))
 
-    a_stack[...] = jnp.zeros(a_stack.shape, F32)
-    b_stack[...] = jnp.zeros(b_stack.shape, F32)
-    kw = lax.broadcasted_iota(jnp.int32, (k_count, width), 0)
-    coef = jnp.zeros((k_count, width), F32)
+    coef = jnp.zeros((8, width), F32)
     for k in range(k_count):
-        coef = jnp.where(kw == k, sigma[k] * LOG2E, coef)
+        coef = jnp.where(row8 == k, sigma[k] * LOG2E, coef)
+    ready(slice(2, 4))
+    for source, rows in ((chars, chars_rows), (draws, draws_rows)):
+        rows[...] = jnp.zeros(rows.shape, F32)
+        for k in range(k_count):
+            for base in range(0, total, 8):
+                for t in range(rows.shape[0]):
+                    part = source[k, base : base + 8, t * LANES : (t + 1) * LANES]
+                    rows[t, pl.ds(base * 8 + k, 8, stride=8), :] = part
 
     def put_stack(ref, g, parts):
         for i, part in enumerate(parts):
-            ref[g, 8 * i : 8 * i + k_count, :] = part
+            ref[g, 8 * i : 8 * i + 8, : part.shape[1]] = part
 
     def build(n, market, g):
-        a1, a2, a3 = three_parts(chars[market] * coef)
-        b1, b2, b3 = three_parts(draws[market])
+        rows = pl.ds(pl.multiple_of(market * 8, 8), 8)
+        a = jnp.concatenate([chars_rows[t, rows, :] for t in range(n // LANES)], axis=1)
+        b = jnp.concatenate([draws_rows[t, rows, :] for t in range(people // LANES)], axis=1)
+        a1, a2, a3 = three_parts(a * coef[:, :n])
+        b1, b2, b3 = three_parts(b)
         put_stack(a_stack, g, (a1, a1, a2, a1, a2, a3))
         put_stack(b_stack, g, (b1, b2, b1, b3, b2, b1))
         a_t = jnp.transpose(a_stack[g, :, :n], (1, 0)).astype(BF)
@@ -185,32 +208,38 @@
     def run_group(n, base):
         ids = [order[base + g] for g in range(GROUP)]
         busy = [1 - converged[i] for i in ids]
-        iters = 2 + TAIL_ITERS * functools.reduce(jnp.maximum, busy)
+        trips = 1 + TAIL_ITERS // 2 * functools.reduce(jnp.maximum, busy)
         for g in range(GROUP):
             build(n, ids[g], g)
         pairs = range(GROUP // 2)
         goals = [by_turns(goal[ids[2 * p], :, :n], goal[ids[2 * p + 1], :, :n]) for p in pairs]
         firsts = [by_turns(first[ids[2 * p], :, :n], first[ids[2 * p + 1], :, :n]) for p in pairs]
 
-        def step(it, carry):
+        def step(state):
             weights = []
             for p in pairs:
-                e = hi_lo_rows(carry[p])
+                e = hi_lo_rows(state[p])
                 inside = by_turns(dot(e, table[2 * p, :n, :]), dot(e, table[2 * p + 1, :n, :]))
                 weights.append(hi_lo_rows(LIFT / (1.0 + add_halves(inside))))
-            out = []
+            sums = []
             for p in pairs:
                 y = dot(weights[p], table_t[p, :, : 2 * n])
-                q = add_halves(by_turns(y[:, :n], y[:, n:]))
+                sums.append(add_halves(by_turns(y[:, :n], y[:, n:])))
+            return sums
+
+        def two_steps(trip, state):
+            sums = step(state)
+            sums = step([goals[p] / sums[p] for p in pairs])
+            for p in pairs:
+                q = sums[p]
                 other = pltpu.roll(q, 1, 0)
                 for g, rows in ((2 * p, by_turns(q, other)), (2 * p + 1, by_turns(other, q))):
-                    q_two[jnp.where(it == 1, ids[g], total), :, :n] = rows
-                    keep = jnp.logical_or(it < 2, busy[g] == 1)
+                    q_two[jnp.where(trip == 0, ids[g], total), :, :n] = rows
+                    keep = jnp.logical_or(trip == 0, busy[g] == 1)
                     q_last[jnp.where(keep, ids[g], total), :, :n] = rows
-                out.append(goals[p] / q)
-            return tuple(out)
-
-        lax.fori_loop(0, iters, step, tuple(firsts))
+            return tuple(goals[p] / sums[p] for p in pairs)
+
+        lax.fori_loop(0, trips, two_steps, tuple(firsts))
 
     def one_group(j, _):
         base = j * GROUP
@@ -245,6 +274,8 @@
 
 def scratch_for(total, width, people):
     return [
+        pltpu.VMEM((width // LANES, total * 8, LANES), F32),
+        pltpu.VMEM((people // LANES, total * 8, LANES), F32),
         pltpu.VMEM((GROUP, 48, width), F32),
         pltpu.VMEM((GROUP, 48, people), F32),
         pltpu.VMEM((GROUP, width, people), BF),
@@ -265,6 +296,7 @@
     people = draws.shape[2]
     smem = pl.BlockSpec(memory_space=pltpu.SMEM)
     vmem = pl.BlockSpec(memory_space=pltpu.VMEM)
+    hbm = pl.BlockSpec(memory_space=pltpu.HBM)
     return pl.pallas_call(
         functools.partial(early_kernel, slots=slots),
         out_shape=(
@@ -272,11 +304,18 @@
             jax.ShapeDtypeStruct((devices, 1, width + LANES), F32),
             jax.ShapeDtypeStruct((total,), jnp.int32),
         ),
-        in_specs=[smem] * 4 + [vmem] * 4,
+        in_specs=[smem] * 4 + [hbm] * 4,
         out_specs=(vmem, vmem, smem),
-        scratch_shapes=[pltpu.SMEM((2 * width // LANES,), jnp.int32)]
+        scratch_shapes=[
+            pltpu.SMEM((2 * width // LANES,), jnp.int32),
+            pltpu.VMEM(start_offset.shape, F32),
+            pltpu.VMEM(chars.shape, F32),
+            pltpu.VMEM(share_rel.shape, F32),
+            pltpu.VMEM(draws.shape, F32),
+            pltpu.SemaphoreType.DMA((4,)),
+        ]
         + scratch_for(total, width, people),
-        compiler_params=pltpu.CompilerParams(vmem_limit_bytes=48 * 2**20),
+        compiler_params=pltpu.CompilerParams(vmem_limit_bytes=60 * 2**20),
         name="early_markets",
     )(sigma, counts, converged, destination, start_offset, chars, share_rel, draws)
 
@@ -296,7 +335,7 @@
         out_specs=vmem,
         scratch_shapes=[pltpu.SMEM((total,), jnp.int32)] + scratch_for(total, width, people),
         input_output_aliases={8: 0},
-        compiler_params=pltpu.CompilerParams(vmem_limit_bytes=48 * 2**20),
+        compiler_params=pltpu.CompilerParams(vmem_limit_bytes=16 * 2**20),
         cost_estimate=pl.CostEstimate(
             flops=rest * width * people * 20,
             bytes_accessed=2 * 2**20,
@@ -306,10 +345,47 @@
     )(sigma, counts, converged, order, start_offset, chars, share_rel, draws, early)
 
 
+def unpack_kernel(core, values, work, norm, *, cores):
+    devices, _, width = values.shape
+    width -= LANES
+    slots = work.shape[0]
+    row = lax.broadcasted_iota(jnp.int32, (slots, LANES), 0).astype(F32)
+    acc = [jnp.zeros((slots, LANES), F32) for _ in range(width // LANES)]
+    for chip in range(devices // cores):
+        source = chip * cores + core[0]
+        named = row == values[source, :, width : width + 1]
+        for t in range(width // LANES):
+            part = values[source, :, t * LANES : (t + 1) * LANES]
+            acc[t] = jnp.where(named, jnp.broadcast_to(part, (slots, LANES)), acc[t])
+    for t in range(width // LANES):
+        work[:, t * LANES : (t + 1) * LANES] = acc[t]
+    sums = [values[d, :, width:] for d in range(devices)]
+    while len(sums) > 1:
+        sums = [a + b for a, b in zip(sums[::2], sums[1::2])]
+    norm[...] = jnp.sqrt(sums[0][:, 1:2] / sums[0][:, 2:3])
+
+
+def unpack(core, values, cores, slots):
+    devices, _, width = values.shape
+    vmem = pl.BlockSpec(memory_space=pltpu.VMEM)
+    return pl.pallas_call(
+        functools.partial(unpack_kernel, cores=cores),
+        out_shape=(
+            jax.ShapeDtypeStruct((slots, width - LANES), F32),
+            jax.ShapeDtypeStruct((1, 1), F32),
+        ),
+        in_specs=[pl.BlockSpec(memory_space=pltpu.SMEM), vmem],
+        out_specs=(vmem, vmem),
+        compiler_params=pltpu.CompilerParams(vmem_limit_bytes=4 * 2**20),
+        name="unpack",
+    )(core, values)
+
+
 def local(start_offset, chars, share_rel, draws, sigma, counts, converged, destination):
     market_count, width = start_offset.shape
     devices = lax.axis_size(CHIP_CORES)
     slots = 3 * market_count // 8
+    chars, draws = jnp.transpose(chars, (1, 0, 2)), jnp.transpose(draws, (1, 0, 2))
     early, send, order = early_markets(
         sigma, counts, converged, destination, start_offset, chars, share_rel, draws,
         devices=devices, slots=slots,
@@ -318,11 +394,10 @@
     delta = late_markets(
         sigma, counts, converged, order, start_offset, chars, share_rel, draws, early
     )
-    values = values.reshape(devices, width + LANES)
-    named = jnp.arange(slots, dtype=F32)[:, None, None] == values[None, :, width : width + 1]
-    work_delta = jnp.sum(jnp.where(named, values[None, :, :width], 0.0), axis=1)
-    totals = jnp.sum(values[:, width + 1 : width + 3], axis=0)
-    return delta, work_delta, jnp.sqrt(totals[0] / totals[1])
+    work_delta, norm = unpack(
+        jnp.full((1,), lax.axis_index("cores"), jnp.int32), values, lax.axis_size("cores"), slots
+    )
+    return delta, work_delta, norm[0, 0]
 
 
 def solution(mesh):

time: 65.4 us -> 57.5 us (0.88)
  starting transfers between devices: 23.1 us -> 17.8 us
  Pallas kernels: 30 us -> 34.3 us
  between operations: 3.26 us -> 0.75 us
  local copies, waits for them, and re-layouts: 2.88 us -> 0.65 us
  other arithmetic: 1.08 us -> 0 us
    all_to_all x1, starting transfers between devices: 23.1 us -> 17.8 us  [local(): lax.all_to_all(send, CHIP_CORES, split_axis=0, concat_axis=0, tiled=True)]
    pallas_call x1, Pallas kernels: 22.3 us -> 26 us  [early_markets(): pl.pallas_call(functools.partial(early_kernel, slots=slots), out_shape=(j...]
    unnamed x17 -> x16, local copies, waits for them, and re-layouts: 2.15 us -> 0.65 us
    reduce_sum x2 -> x0, other arithmetic: 1.07 us -> none  [the longest x1 0.97 us: local(): work_delta = jnp.sum(jnp.where(named, values[None, :, :width], 0.0), axis=1)]
    pallas_call x0 -> x1, Pallas kernels: none -> 0.76 us  [unpack(): pl.pallas_call(functools.partial(unpack_kernel, cores=cores), out_shape=(...]
    slice x3 -> x0, local copies, waits for them, and re-layouts: 0.72 us -> none  [the longest x1 0.59 us: local(): return (delta, work_delta, jnp.sqrt(totals[0] / totals[1]))]
  transfers between devices with their start and end apart: 1 -> 1, of which waited for: 1 -> 1; matrix products, arithmetic and copies ran while one was open for 0% -> 0% of each run, Pallas kernels for 12% -> 13%
where the time goes in v3:
time: 57.5 us; the launch traced here: 57.2 us
  Pallas kernels  34.3 us (60%)
  starting transfers between devices  17.8 us (31%)
  waiting for transfers between devices  3.79 us (7%)
  between operations  0.75 us (1%)
  local copies, waits for them, and re-layouts  0.65 us (1%)
    pallas_call x1, Pallas kernels, early_markets(): pl.pallas_call(functools.partial(early_kernel, slots=slots), out_shape=(j...  26 us
    all_to_all x1, starting transfers between devices, local(): lax.all_to_all(send, CHIP_CORES, split_axis=0, concat_axis=0, tiled=True)  17.8 us
    pallas_call x1, Pallas kernels, late_markets(): pl.pallas_call(late_kernel, out_shape=jax.ShapeDtypeStruct((total, width)...  7.5 us
    all_to_all x1, waiting for transfers between devices, local(): lax.all_to_all(send, CHIP_CORES, split_axis=0, concat_axis=0, tiled=True)  3.79 us
  transfers between devices with their start and end apart: 1, of which 1 were waited for; matrix products, arithmetic and copies ran while one was open for 0% of the time, Pallas kernels for 13%

profile of v3, /device:TPU:1, one launch (start us, length us, event | category | flops | bytes accessed | tf_op | source)
XLA Modules:
  0.0 57.2 jit_solution(1595379143523684213)
XLA Ops:
  0.6 0.0 copy-start.1
  0.6 0.0 copy-start.3
  0.7 26.0 %early_markets.1 = (f32[32,512]{1,0:T(8,128)}, f32[128,1,640]{2,1,0:T(1,128)}, s32[32]{0:T(128)}) custom-call(f32[6]{0:T(128)} %sigma.3, s32[32]{0:T(128)} %counts.3, s32[32]{0:T(128)} %converged.3, s32[32]{0:T(128)} %destination.1, f32[32,512]{1,0:T(8,128)} %start.3, f32[6,32,512]{2,1,0:T(8,128)} %bitcast.6, f32[32,512]{1,0:T(8,128)} %share.3, ...), custom_call_target="tpu_custom_call" | custom-call | tf_op jit(solution)/shard_map/early_markets/pallas_call | solution.py:300
  26.7 0.0 copy-start
  26.7 0.0 copy-start.2
  26.7 17.8 %all-to-all-start = ((f32[128,1,640]{2,1,0:T(1,128)}), f32[128,1,640]{2,1,0:T(1,128)S(1)}, u32[]{:S(2)}, u32[]{:S(2)}) async-start(f32[128,1,640]{2,1,0:T(1,128)} %get-tuple-element.10), calls=%async_computation | async-start | bytes 655360 | tf_op jit(solution)/shard_map/all_to_all | solution.py:393
  44.5 0.0 copy-start.7
  44.5 0.0 copy-start.4
  44.5 0.0 copy-start.5
  44.5 0.0 copy-start.6
  44.5 0.0 copy-done.1
  44.5 0.0 copy-done.3
  44.5 0.0 copy-done
  44.5 0.0 copy-done.2
  44.6 0.6 copy-done.7
  45.1 0.0 copy-done.4
  45.1 0.0 copy-done.5
  45.2 0.0 copy-done.6
  45.2 7.5 %late_markets.1 = f32[32,512]{1,0:T(8,128)} custom-call(f32[6]{0:T(128)S(1)} %copy-done.4, s32[32]{0:T(128)S(1)} %copy-done.5, s32[32]{0:T(128)S(1)} %copy-done.6, s32[32]{0:T(128)S(1)} %copy-done.7, f32[32,512]{1,0:T(8,128)S(1)} %copy-done.2, f32[6,32,512]{2,1,0:T(8,128)S(1)} %bitcast.7, f32[32,512]{1,0:T(8,128)S(1)} %copy-done.3, ...), custom_call_target="tpu_custom_call", output_to_operand_aliasing={{}: (8, {})} | custom-call | flops 94371840 | bytes 2097152 | tf_op jit(solution)/shard_map/late_markets/pallas_call | solution.py:331
  52.7 3.8 %all-to-all-done.values = f32[128,1,640]{2,1,0:T(1,128)S(1)} async-done(((f32[128,1,640]{2,1,0:T(1,128)}), f32[128,1,640]{2,1,0:T(1,128)S(1)}, u32[]{:S(2)}, u32[]{:S(2)}) %all-to-all-start) | async-done | bytes 327712 | tf_op jit(solution)/shard_map/all_to_all | solution.py:393
  56.5 0.8 %unpack.1 = (f32[12,512]{1,0:T(8,128)}, f32[1,1]{1,0:T(1,128)}) custom-call(s32[1]{0:T(128)} %bitcast.2.core, f32[128,1,640]{2,1,0:T(1,128)S(1)} %all-to-all-done.values), custom_call_target="tpu_custom_call" | custom-call | tf_op jit(solution)/shard_map/unpack/pallas_call | solution.py:371
Async XLA Ops:
  0.6 43.9 %copy-start.1 = (f32[32,6,512]{2,0,1:T(8,128)S(1)}, f32[32,6,512]{2,0,1:T(8,128)}, u32[]{:S(2)}) copy-start(f32[32,6,512]{2,0,1:T(8,128)} %param.9) | copy-start | bytes 1179652
  0.6 43.9 %copy-start.3 = (f32[32,512]{1,0:T(8,128)S(1)}, f32[32,512]{1,0:T(8,128)}, u32[]{:S(2)}) copy-start(f32[32,512]{1,0:T(8,128)} %share.3) | copy-start | bytes 196612
  26.7 17.9 %copy-start = (f32[32,6,768]{2,0,1:T(8,128)S(1)}, f32[32,6,768]{2,0,1:T(8,128)}, u32[]{:S(2)}) copy-start(f32[32,6,768]{2,0,1:T(8,128)} %param.11) | copy-start | bytes 1769476
  26.7 17.9 %copy-start.2 = (f32[32,512]{1,0:T(8,128)S(1)}, f32[32,512]{1,0:T(8,128)}, u32[]{:S(2)}) copy-start(f32[32,512]{1,0:T(8,128)} %start.3) | copy-start | bytes 196612
  26.7 29.8 %all-to-all-start = ((f32[128,1,640]{2,1,0:T(1,128)}), f32[128,1,640]{2,1,0:T(1,128)S(1)}, u32[]{:S(2)}, u32[]{:S(2)}) async-start(f32[128,1,640]{2,1,0:T(1,128)} %get-tuple-element.10), calls=%async_computation | async-start | bytes 655360 | tf_op jit(solution)/shard_map/all_to_all | solution.py:393
  44.5 0.7 %copy-start.7 = (s32[32]{0:T(128)S(1)}, s32[32]{0:T(128)}, u32[]{:S(2)}) copy-start(s32[32]{0:T(128)} %get-tuple-element.8.order) | copy-start | bytes 388
  44.5 0.7 %copy-start.4 = (f32[6]{0:T(128)S(1)}, f32[6]{0:T(128)}, u32[]{:S(2)}) copy-start(f32[6]{0:T(128)} %sigma.3) | copy-start | bytes 76
  44.5 0.7 %copy-start.5 = (s32[32]{0:T(128)S(1)}, s32[32]{0:T(128)}, u32[]{:S(2)}) copy-start(s32[32]{0:T(128)} %counts.3) | copy-start | bytes 388
  44.5 0.7 %copy-start.6 = (s32[32]{0:T(128)S(1)}, s32[32]{0:T(128)}, u32[]{:S(2)}) copy-start(s32[32]{0:T(128)} %converged.3) | copy-start | bytes 388

commit v4 on v3

--- a/solution.py
+++ b/solution.py
@@ -12,6 +12,7 @@
 TAIL_ITERS = 4
 CHIP_CORES = ("chip_0", "chip_1", "chip_2", "cores")
 
+SIDE = 256
 GROUP = 4
 EARLY = 20
 LANES = 128
@@ -58,7 +59,7 @@
         bucket_at[b] = bucket_at[b] + 1
         return active + jnp.where(converged[i] == 0, counts[i], 0)
 
-    active = lax.fori_loop(0, total, tally, jnp.int32(0))
+    active = lax.fori_loop(0, total, tally, jnp.int32(0), unroll=True)
     at = jnp.int32(0)
     for b in range(2 * tiles):
         size = bucket_at[b]
@@ -71,7 +72,7 @@
         bucket_at[b] = bucket_at[b] + 1
         return 0
 
-    lax.fori_loop(0, total, put, 0)
+    lax.fori_loop(0, total, put, 0, unroll=True)
     return active
 
 
@@ -212,20 +213,38 @@
         for g in range(GROUP):
             build(n, ids[g], g)
         pairs = range(GROUP // 2)
+        by_matrix = people - SIDE
         goals = [by_turns(goal[ids[2 * p], :, :n], goal[ids[2 * p + 1], :, :n]) for p in pairs]
         firsts = [by_turns(first[ids[2 * p], :, :n], first[ids[2 * p + 1], :, :n]) for p in pairs]
 
         def step(state):
             weights = []
+            sides = []
             for p in pairs:
                 e = hi_lo_rows(state[p])
                 inside = by_turns(dot(e, table[2 * p, :n, :]), dot(e, table[2 * p + 1, :n, :]))
-                weights.append(hi_lo_rows(LIFT / (1.0 + add_halves(inside))))
+                weight = LIFT / (1.0 + add_halves(inside))
+                weights.append(hi_lo_rows(weight[:, :by_matrix]))
+                sides.append([side_sum(p, h, n, weight) for h in range(2)])
             sums = []
             for p in pairs:
-                y = dot(weights[p], table_t[p, :, : 2 * n])
-                sums.append(add_halves(by_turns(y[:, :n], y[:, n:])))
+                y = dot(weights[p], table_t[p, :by_matrix, : 2 * n])
+                y = by_turns(y[:, :n] + sides[p][0], y[:, n:] + sides[p][1])
+                sums.append(add_halves(y))
             return sums
+
+        def side_sum(p, h, n, weight):
+            total8 = jnp.zeros((8, n), F32)
+            for r0 in range(by_matrix, people, LANES):
+                row = jnp.broadcast_to(weight[h : h + 1, r0 : r0 + LANES], (LANES, LANES))
+                column = jnp.transpose(row, (1, 0))
+                block = table_t[p, r0 : r0 + LANES, h * n : (h + 1) * n].astype(F32)
+                for r in range(0, LANES, 8):
+                    w = column[r : r + 8]
+                    w = jnp.concatenate([w] * (n // LANES), axis=1)
+                    total8 = total8 + block[r : r + 8] * w
+            total8 = total8 + pltpu.roll(total8, 2, 0)
+            return total8 + pltpu.roll(total8, 1, 0)
 
         def two_steps(trip, state):
             sums = step(state)

time: 57.5 us -> 55.1 us (0.958)
  Pallas kernels: 34.3 us -> 28.5 us
  starting transfers between devices: 17.8 us -> 19.7 us
  waiting for transfers between devices: 3.79 us -> 5.01 us
    pallas_call x1, Pallas kernels: 26 us -> 21.4 us  [early_markets(): pl.pallas_call(functools.partial(early_kernel, slots=slots), out_shape=(j...]
    all_to_all x1, starting transfers between devices: 17.8 us -> 19.7 us  [local(): lax.all_to_all(send, CHIP_CORES, split_axis=0, concat_axis=0, tiled=True)]
    pallas_call x1, Pallas kernels: 7.5 us -> 6.28 us  [late_markets(): pl.pallas_call(late_kernel, out_shape=jax.ShapeDtypeStruct((total, width)...]
    all_to_all x1, waiting for transfers between devices: 3.79 us -> 5.01 us  [local(): lax.all_to_all(send, CHIP_CORES, split_axis=0, concat_axis=0, tiled=True)]
  transfers between devices with their start and end apart: 1 -> 1, of which waited for: 1 -> 1; matrix products, arithmetic and copies ran while one was open for 0% -> 0% of each run, Pallas kernels for 13% -> 12%
where the time goes in v4:
time: 55.1 us; the launch traced here: 54.6 us
  Pallas kernels  28.5 us (52%)
  starting transfers between devices  19.7 us (36%)
  waiting for transfers between devices  5.01 us (9%)
  between operations  0.75 us (1%)
  local copies, waits for them, and re-layouts  0.65 us (1%)
    pallas_call x1, Pallas kernels, early_markets(): pl.pallas_call(functools.partial(early_kernel, slots=slots), out_shape=(j...  21.4 us
    all_to_all x1, starting transfers between devices, local(): lax.all_to_all(send, CHIP_CORES, split_axis=0, concat_axis=0, tiled=True)  19.7 us
    pallas_call x1, Pallas kernels, late_markets(): pl.pallas_call(late_kernel, out_shape=jax.ShapeDtypeStruct((total, width)...  6.28 us
    all_to_all x1, waiting for transfers between devices, local(): lax.all_to_all(send, CHIP_CORES, split_axis=0, concat_axis=0, tiled=True)  5.01 us
  transfers between devices with their start and end apart: 1, of which 1 were waited for; matrix products, arithmetic and copies ran while one was open for 0% of the time, Pallas kernels for 12%

profile of v4, /device:TPU:1, one launch (start us, length us, event | category | flops | bytes accessed | tf_op | source)
XLA Modules:
  0.0 54.6 jit_solution(2332645918551502824)
XLA Ops:
  0.6 0.0 copy-start.1
  0.6 0.0 copy-start.3
  0.7 21.4 %early_markets.1 = (f32[32,512]{1,0:T(8,128)}, f32[128,1,640]{2,1,0:T(1,128)}, s32[32]{0:T(128)}) custom-call(f32[6]{0:T(128)} %sigma.3, s32[32]{0:T(128)} %counts.3, s32[32]{0:T(128)} %converged.3, s32[32]{0:T(128)} %destination.1, f32[32,512]{1,0:T(8,128)} %start.3, f32[6,32,512]{2,1,0:T(8,128)} %bitcast.6, f32[32,512]{1,0:T(8,128)} %share.3, ...), custom_call_target="tpu_custom_call" | custom-call | tf_op jit(solution)/shard_map/early_markets/pallas_call | solution.py:319
  22.1 0.0 copy-start
  22.1 0.0 copy-start.2
  22.1 19.7 %all-to-all-start = ((f32[128,1,640]{2,1,0:T(1,128)}), f32[128,1,640]{2,1,0:T(1,128)S(1)}, u32[]{:S(2)}, u32[]{:S(2)}) async-start(f32[128,1,640]{2,1,0:T(1,128)} %get-tuple-element.10), calls=%async_computation | async-start | bytes 655360 | tf_op jit(solution)/shard_map/all_to_all | solution.py:412
  41.8 0.0 copy-start.7
  41.9 0.0 copy-start.4
  41.9 0.0 copy-start.5
  41.9 0.0 copy-start.6
  41.9 0.0 copy-done.1
  41.9 0.0 copy-done.3
  41.9 0.0 copy-done
  41.9 0.0 copy-done.2
  41.9 0.6 %copy-done.7 = s32[32]{0:T(128)S(1)} copy-done((s32[32]{0:T(128)S(1)}, s32[32]{0:T(128)}, u32[]{:S(2)}) %copy-start.7) | copy-done | bytes 152
  42.5 0.0 copy-done.4
  42.5 0.0 copy-done.5
  42.5 0.0 copy-done.6
  42.6 6.3 %late_markets.1 = f32[32,512]{1,0:T(8,128)} custom-call(f32[6]{0:T(128)S(1)} %copy-done.4, s32[32]{0:T(128)S(1)} %copy-done.5, s32[32]{0:T(128)S(1)} %copy-done.6, s32[32]{0:T(128)S(1)} %copy-done.7, f32[32,512]{1,0:T(8,128)S(1)} %copy-done.2, f32[6,32,512]{2,1,0:T(8,128)S(1)} %bitcast.7, f32[32,512]{1,0:T(8,128)S(1)} %copy-done.3, ...), custom_call_target="tpu_custom_call", output_to_operand_aliasing={{}: (8, {})} | custom-call | flops 94371840 | bytes 2097152 | tf_op jit(solution)/shard_map/late_markets/pallas_call | solution.py:350
  48.8 5.0 %all-to-all-done.values = f32[128,1,640]{2,1,0:T(1,128)S(1)} async-done(((f32[128,1,640]{2,1,0:T(1,128)}), f32[128,1,640]{2,1,0:T(1,128)S(1)}, u32[]{:S(2)}, u32[]{:S(2)}) %all-to-all-start) | async-done | bytes 327712 | tf_op jit(solution)/shard_map/all_to_all | solution.py:412
  53.8 0.8 %unpack.1 = (f32[12,512]{1,0:T(8,128)}, f32[1,1]{1,0:T(1,128)}) custom-call(s32[1]{0:T(128)} %bitcast.2.core, f32[128,1,640]{2,1,0:T(1,128)S(1)} %all-to-all-done.values), custom_call_target="tpu_custom_call" | custom-call | tf_op jit(solution)/shard_map/unpack/pallas_call | solution.py:390
Async XLA Ops:
  0.6 41.3 %copy-start.1 = (f32[32,6,512]{2,0,1:T(8,128)S(1)}, f32[32,6,512]{2,0,1:T(8,128)}, u32[]{:S(2)}) copy-start(f32[32,6,512]{2,0,1:T(8,128)} %param.9) | copy-start | bytes 1179652
  0.6 41.3 %copy-start.3 = (f32[32,512]{1,0:T(8,128)S(1)}, f32[32,512]{1,0:T(8,128)}, u32[]{:S(2)}) copy-start(f32[32,512]{1,0:T(8,128)} %share.3) | copy-start | bytes 196612
  22.1 19.8 %copy-start = (f32[32,6,768]{2,0,1:T(8,128)S(1)}, f32[32,6,768]{2,0,1:T(8,128)}, u32[]{:S(2)}) copy-start(f32[32,6,768]{2,0,1:T(8,128)} %param.11) | copy-start | bytes 1769476
  22.1 19.8 %copy-start.2 = (f32[32,512]{1,0:T(8,128)S(1)}, f32[32,512]{1,0:T(8,128)}, u32[]{:S(2)}) copy-start(f32[32,512]{1,0:T(8,128)} %start.3) | copy-start | bytes 196612
  22.1 31.7 %all-to-all-start = ((f32[128,1,640]{2,1,0:T(1,128)}), f32[128,1,640]{2,1,0:T(1,128)S(1)}, u32[]{:S(2)}, u32[]{:S(2)}) async-start(f32[128,1,640]{2,1,0:T(1,128)} %get-tuple-element.10), calls=%async_computation | async-start | bytes 655360 | tf_op jit(solution)/shard_map/all_to_all | solution.py:412
  41.8 0.7 %copy-start.7 = (s32[32]{0:T(128)S(1)}, s32[32]{0:T(128)}, u32[]{:S(2)}) copy-start(s32[32]{0:T(128)} %get-tuple-element.8.order) | copy-start | bytes 388
  41.9 0.7 %copy-start.4 = (f32[6]{0:T(128)S(1)}, f32[6]{0:T(128)}, u32[]{:S(2)}) copy-start(f32[6]{0:T(128)} %sigma.3) | copy-start | bytes 76
  41.9 0.7 %copy-start.5 = (s32[32]{0:T(128)S(1)}, s32[32]{0:T(128)}, u32[]{:S(2)}) copy-start(s32[32]{0:T(128)} %counts.3) | copy-start | bytes 388
  41.9 0.7 %copy-start.6 = (s32[32]{0:T(128)S(1)}, s32[32]{0:T(128)}, u32[]{:S(2)}) copy-start(s32[32]{0:T(128)} %converged.3) | copy-start | bytes 388

commit v5 on v4

--- a/solution.py
+++ b/solution.py
@@ -98,7 +98,7 @@
     active = sort_markets(counts, converged, order, bucket_at, total, width // LANES)
     final_rows = run_markets(
         sigma, counts, converged, start_here, chars_here, share_here, draws_here, order, *scratch,
-        0, EARLY, ready,
+        0, EARLY, True, ready,
     )
     row8 = lax.broadcasted_iota(jnp.int32, (8, width), 0)
     acc = jnp.zeros((8, width), F32)
@@ -149,7 +149,7 @@
 def run_markets(
     sigma, counts, converged, start, chars, share, draws, order,
     chars_rows, draws_rows, a_stack, b_stack, table, table_t, log_obs, goal, first, q_two, q_last,
-    begin, end, ready=lambda which: None,
+    begin, end, tail=False, ready=lambda which: None,
 ):
     total, width = start.shape
     people = draws.shape[2]
@@ -209,7 +209,6 @@
     def run_group(n, base):
         ids = [order[base + g] for g in range(GROUP)]
         busy = [1 - converged[i] for i in ids]
-        trips = 1 + TAIL_ITERS // 2 * functools.reduce(jnp.maximum, busy)
         for g in range(GROUP):
             build(n, ids[g], g)
         pairs = range(GROUP // 2)
@@ -246,19 +245,28 @@
             total8 = total8 + pltpu.roll(total8, 2, 0)
             return total8 + pltpu.roll(total8, 1, 0)
 
-        def two_steps(trip, state):
-            sums = step(state)
-            sums = step([goals[p] / sums[p] for p in pairs])
-            for p in pairs:
-                q = sums[p]
+        def steps(count, state):
+            for it in range(count):
+                sums = step(state)
+                state = [goals[p] / sums[p] for p in pairs]
+            rows = []
+            for q in sums:
                 other = pltpu.roll(q, 1, 0)
-                for g, rows in ((2 * p, by_turns(q, other)), (2 * p + 1, by_turns(other, q))):
-                    q_two[jnp.where(trip == 0, ids[g], total), :, :n] = rows
-                    keep = jnp.logical_or(trip == 0, busy[g] == 1)
-                    q_last[jnp.where(keep, ids[g], total), :, :n] = rows
-            return tuple(goals[p] / sums[p] for p in pairs)
-
-        lax.fori_loop(0, trips, two_steps, tuple(firsts))
+                rows += [by_turns(q, other), by_turns(other, q)]
+            return state, rows
+
+        state, rows = steps(2, firsts)
+        for g in range(GROUP):
+            q_two[ids[g], :, :n] = rows[g]
+            q_last[ids[g], :, :n] = rows[g]
+        if not tail:
+            return
+
+        @pl.when(functools.reduce(jnp.maximum, busy) == 1)
+        def _():
+            _, rows = steps(TAIL_ITERS, state)
+            for g in range(GROUP):
+                q_last[jnp.where(busy[g] == 1, ids[g], total), :, :n] = rows[g]
 
     def one_group(j, _):
         base = j * GROUP

time: 55.1 us -> 54.5 us (0.989)
  Pallas kernels: 28.5 us -> 26.5 us
  starting transfers between devices: 19.7 us -> 20.7 us
  waiting for transfers between devices: 5.01 us -> 5.61 us
    pallas_call x1, Pallas kernels: 21.4 us -> 20 us  [early_markets(): pl.pallas_call(functools.partial(early_kernel, slots=slots), out_shape=(j...]
    all_to_all x1, starting transfers between devices: 19.7 us -> 20.7 us  [local(): lax.all_to_all(send, CHIP_CORES, split_axis=0, concat_axis=0, tiled=True)]
    all_to_all x1, waiting for transfers between devices: 5.01 us -> 5.61 us  [local(): lax.all_to_all(send, CHIP_CORES, split_axis=0, concat_axis=0, tiled=True)]
    pallas_call x1, Pallas kernels: 6.28 us -> 5.69 us  [late_markets(): pl.pallas_call(late_kernel, out_shape=jax.ShapeDtypeStruct((total, width)...]
  transfers between devices with their start and end apart: 1 -> 1, of which waited for: 1 -> 1; matrix products, arithmetic and copies ran while one was open for 0% -> 0% of each run, Pallas kernels for 12% -> 10%
where the time goes in v5:
time: 54.5 us; the launch traced here: 54.2 us
  Pallas kernels  26.5 us (49%)
  starting transfers between devices  20.7 us (38%)
  waiting for transfers between devices  5.61 us (10%)
  between operations  0.75 us (1%)
  local copies, waits for them, and re-layouts  0.65 us (1%)
    all_to_all x1, starting transfers between devices, local(): lax.all_to_all(send, CHIP_CORES, split_axis=0, concat_axis=0, tiled=True)  20.7 us
    pallas_call x1, Pallas kernels, early_markets(): pl.pallas_call(functools.partial(early_kernel, slots=slots), out_shape=(j...  20 us
    pallas_call x1, Pallas kernels, late_markets(): pl.pallas_call(late_kernel, out_shape=jax.ShapeDtypeStruct((total, width)...  5.69 us
    all_to_all x1, waiting for transfers between devices, local(): lax.all_to_all(send, CHIP_CORES, split_axis=0, concat_axis=0, tiled=True)  5.61 us
  transfers between devices with their start and end apart: 1, of which 1 were waited for; matrix products, arithmetic and copies ran while one was open for 0% of the time, Pallas kernels for 10%

profile of v5, /device:TPU:1, one launch (start us, length us, event | category | flops | bytes accessed | tf_op | source)
XLA Modules:
  0.0 54.2 jit_solution(13081776549481677907)
XLA Ops:
  0.6 0.0 copy-start.1
  0.6 0.0 copy-start.3
  0.7 20.0 %early_markets.1 = (f32[32,512]{1,0:T(8,128)}, f32[128,1,640]{2,1,0:T(1,128)}, s32[32]{0:T(128)}) custom-call(f32[6]{0:T(128)} %sigma.3, s32[32]{0:T(128)} %counts.3, s32[32]{0:T(128)} %converged.3, s32[32]{0:T(128)} %destination.1, f32[32,512]{1,0:T(8,128)} %start.3, f32[6,32,512]{2,1,0:T(8,128)} %bitcast.6, f32[32,512]{1,0:T(8,128)} %share.3, ...), custom_call_target="tpu_custom_call" | custom-call | tf_op jit(solution)/shard_map/early_markets/pallas_call | solution.py:327
  20.7 0.0 copy-start
  20.7 0.0 copy-start.2
  20.7 20.7 %all-to-all-start = ((f32[128,1,640]{2,1,0:T(1,128)}), f32[128,1,640]{2,1,0:T(1,128)S(1)}, u32[]{:S(2)}, u32[]{:S(2)}) async-start(f32[128,1,640]{2,1,0:T(1,128)} %get-tuple-element.10), calls=%async_computation | async-start | bytes 655360 | tf_op jit(solution)/shard_map/all_to_all | solution.py:420
  41.4 0.0 copy-start.7
  41.4 0.0 copy-start.4
  41.4 0.0 copy-start.5
  41.5 0.0 copy-start.6
  41.5 0.0 copy-done.1
  41.5 0.0 copy-done.3
  41.5 0.0 copy-done
  41.5 0.0 copy-done.2
  41.5 0.6 %copy-done.7 = s32[32]{0:T(128)S(1)} copy-done((s32[32]{0:T(128)S(1)}, s32[32]{0:T(128)}, u32[]{:S(2)}) %copy-start.7) | copy-done | bytes 152
  42.1 0.0 copy-done.4
  42.1 0.0 copy-done.5
  42.1 0.0 copy-done.6
  42.1 5.7 %late_markets.1 = f32[32,512]{1,0:T(8,128)} custom-call(f32[6]{0:T(128)S(1)} %copy-done.4, s32[32]{0:T(128)S(1)} %copy-done.5, s32[32]{0:T(128)S(1)} %copy-done.6, s32[32]{0:T(128)S(1)} %copy-done.7, f32[32,512]{1,0:T(8,128)S(1)} %copy-done.2, f32[6,32,512]{2,1,0:T(8,128)S(1)} %bitcast.7, f32[32,512]{1,0:T(8,128)S(1)} %copy-done.3, ...), custom_call_target="tpu_custom_call", output_to_operand_aliasing={{}: (8, {})} | custom-call | flops 94371840 | bytes 2097152 | tf_op jit(solution)/shard_map/late_markets/pallas_call | solution.py:358
  47.8 5.6 %all-to-all-done.values = f32[128,1,640]{2,1,0:T(1,128)S(1)} async-done(((f32[128,1,640]{2,1,0:T(1,128)}), f32[128,1,640]{2,1,0:T(1,128)S(1)}, u32[]{:S(2)}, u32[]{:S(2)}) %all-to-all-start) | async-done | bytes 327712 | tf_op jit(solution)/shard_map/all_to_all | solution.py:420
  53.4 0.8 %unpack.1 = (f32[12,512]{1,0:T(8,128)}, f32[1,1]{1,0:T(1,128)}) custom-call(s32[1]{0:T(128)} %bitcast.2.core, f32[128,1,640]{2,1,0:T(1,128)S(1)} %all-to-all-done.values), custom_call_target="tpu_custom_call" | custom-call | tf_op jit(solution)/shard_map/unpack/pallas_call | solution.py:398
Async XLA Ops:
  0.6 40.8 %copy-start.1 = (f32[32,6,512]{2,0,1:T(8,128)S(1)}, f32[32,6,512]{2,0,1:T(8,128)}, u32[]{:S(2)}) copy-start(f32[32,6,512]{2,0,1:T(8,128)} %param.9) | copy-start | bytes 1179652
  0.6 40.8 %copy-start.3 = (f32[32,512]{1,0:T(8,128)S(1)}, f32[32,512]{1,0:T(8,128)}, u32[]{:S(2)}) copy-start(f32[32,512]{1,0:T(8,128)} %share.3) | copy-start | bytes 196612
  20.7 20.8 %copy-start = (f32[32,6,768]{2,0,1:T(8,128)S(1)}, f32[32,6,768]{2,0,1:T(8,128)}, u32[]{:S(2)}) copy-start(f32[32,6,768]{2,0,1:T(8,128)} %param.11) | copy-start | bytes 1769476
  20.7 20.8 %copy-start.2 = (f32[32,512]{1,0:T(8,128)S(1)}, f32[32,512]{1,0:T(8,128)}, u32[]{:S(2)}) copy-start(f32[32,512]{1,0:T(8,128)} %start.3) | copy-start | bytes 196612
  20.7 32.7 %all-to-all-start = ((f32[128,1,640]{2,1,0:T(1,128)}), f32[128,1,640]{2,1,0:T(1,128)S(1)}, u32[]{:S(2)}, u32[]{:S(2)}) async-start(f32[128,1,640]{2,1,0:T(1,128)} %get-tuple-element.10), calls=%async_computation | async-start | bytes 655360 | tf_op jit(solution)/shard_map/all_to_all | solution.py:420
  41.4 0.7 %copy-start.7 = (s32[32]{0:T(128)S(1)}, s32[32]{0:T(128)}, u32[]{:S(2)}) copy-start(s32[32]{0:T(128)} %get-tuple-element.8.order) | copy-start | bytes 388
  41.4 0.7 %copy-start.4 = (f32[6]{0:T(128)S(1)}, f32[6]{0:T(128)}, u32[]{:S(2)}) copy-start(f32[6]{0:T(128)} %sigma.3) | copy-start | bytes 76
  41.4 0.7 %copy-start.5 = (s32[32]{0:T(128)S(1)}, s32[32]{0:T(128)}, u32[]{:S(2)}) copy-start(s32[32]{0:T(128)} %counts.3) | copy-start | bytes 388
  41.5 0.7 %copy-start.6 = (s32[32]{0:T(128)S(1)}, s32[32]{0:T(128)}, u32[]{:S(2)}) copy-start(s32[32]{0:T(128)} %converged.3) | copy-start | bytes 388
